TPU v7x, 128 devices: a whole 4x4x4 slice. The times are simulated.
128 devices in a mesh: dp: 1, tp: 2 (over core), ep: 64 (over z, y, x).
Axes of the slice: x: 4, y: 4, z: 4, core: 2. Of those that a mesh axis runs over, the one named last changes fastest.
Arguments:
- tokens: bfloat16 [65536, 2048], P(('dp', 'ep'))
- logits: float32 [65536, 128], P(('dp', 'ep'))
- w_up: bfloat16 [128, 2048, 768], P('ep', None, 'tp')
- w_down: bfloat16 [128, 768, 2048], P('ep', 'tp')
Outputs:
- output: bfloat16 [65536, 2048], P(('dp', 'ep'))
All inputs are finite; a program needn't handle non-finite values.
Results may differ from a plain program's by a relative error of at most 0.001.
Values are sent between devices in bfloat16 or wider.
A program may use at most 1 GiB of HBM per device.

v0:
```python
import jax
import jax.numpy as jnp
from jax import lax
from jax.sharding import PartitionSpec as P

CAP_FACTOR = 2


def solution(mesh):
    n_groups = mesh.shape["ep"]

    def local_layer(x_local, logit_local, w_up, w_down):
        shard_len, d_model = x_local.shape
        n_experts = logit_local.shape[1]
        own_experts = w_up.shape[0]
        capacity = CAP_FACTOR * shard_len * n_groups // n_experts
        src_cap = 2 * capacity // n_groups
        gate_all = jax.nn.softmax(logit_local, axis=-1)
        cand_val, cand_idx = lax.top_k(logit_local.T, src_cap)
        recv_val = lax.all_to_all(cand_val.reshape(n_groups, own_experts, src_cap), "ep", 0, 0, tiled=True)
        merged = recv_val.transpose(1, 0, 2).reshape(own_experts, n_groups * src_cap)
        own_thresh = lax.top_k(merged, capacity)[0][:, capacity - 1]
        thresh = lax.all_gather(own_thresh, "ep", tiled=True)
        keep_mask = cand_val >= thresh[:, None]
        send_rows = jnp.take(x_local, cand_idx.reshape(-1), axis=0).reshape(n_groups, own_experts, src_cap, d_model)
        recv_rows = lax.all_to_all(send_rows, "ep", 0, 0, tiled=True)
        is_chosen = (merged >= own_thresh[:, None]).astype(jnp.int32)
        run_count = jnp.cumsum(is_chosen, axis=1)
        targets = jnp.arange(1, capacity + 1, dtype=jnp.int32)
        pick_pos = jax.vmap(lambda run_row: jnp.searchsorted(run_row, targets))(run_count)
        expert_ids = jnp.arange(own_experts, dtype=jnp.int32)[:, None]
        flat_pick = (pick_pos // src_cap) * (own_experts * src_cap) + expert_ids * src_cap + pick_pos % src_cap
        picked = jnp.take(recv_rows.reshape(-1, d_model), flat_pick.reshape(-1), axis=0).reshape(own_experts, capacity, d_model)
        pre_act = jnp.einsum("ecd,edf->ecf", picked, w_up, preferred_element_type=jnp.float32)
        hidden = jax.nn.gelu(pre_act, approximate=True).astype(jnp.bfloat16)
        part_out = jnp.einsum("ecf,efd->ecd", hidden, w_down, preferred_element_type=jnp.float32)
        expert_out = lax.psum(part_out, "tp").astype(jnp.bfloat16)
        slot_rank = jnp.maximum(run_count - 1, 0).reshape(own_experts, n_groups, src_cap).transpose(1, 0, 2)
        back_idx = slot_rank + expert_ids[None] * capacity
        back_rows = jnp.take(expert_out.reshape(-1, d_model), back_idx.reshape(-1), axis=0).reshape(n_groups, own_experts, src_cap, d_model)
        returned = lax.all_to_all(back_rows, "ep", 0, 0, tiled=True).reshape(n_experts, src_cap, d_model)
        gate_sel = jnp.take_along_axis(gate_all.T, cand_idx, axis=1)
        weight = jnp.where(keep_mask, gate_sel, 0.0)
        contrib = returned * weight[:, :, None]
        mix_sum = jax.ops.segment_sum(contrib.reshape(-1, d_model), cand_idx.reshape(-1), num_segments=shard_len)
        return (x_local.astype(jnp.float32) + mix_sum).astype(jnp.bfloat16)

    token_spec = P(("dp", "ep"), None)
    return jax.shard_map(local_layer, mesh=mesh, in_specs=(token_spec, token_spec, P("ep", None, "tp"), P("ep", "tp", None)), out_specs=token_spec, check_vma=False)
```

profile of v0, /device:TPU:2, one launch (start us, length us, event | category | flops | bytes accessed | tf_op | source)
XLA Modules:
  0.0 1015.6 jit_solution(7267007125351280664)
XLA Ops:
  0.8 22.7 %top_k.16 = (f32[128,1024]{0,1:T(8,128)}, s32[128,1024]{0,1:T(8,128)}) sort(f32[128,1024]{0,1:T(8,128)} %bitcast.59, s32[128,1024]{0,1:T(8,128)} %top_k.15.clone), dimensions={1}, to_apply=%region_0.0 | sort | flops 2228224 | bytes 2097152 | tf_op jit(solution)/shard_map/top_k | solution.py:19
  41.6 34.1 %gather_fusion.1 = bf16[4096,2048]{1,0:T(8,128)(2,1)} fusion(bf16[1024,2048]{1,0:T(8,128)(2,1)} %param.6, s32[4096]{0:T(1024)S(1)} %broadcast_clamp_fusion.1), kind=kCustom, calls=%fused_computation.1 | custom fusion | bytes 33570816 | tf_op jit(solution)/shard_map/jit(_take)/gather | solution.py:25
  75.7 14.1 %broadcast_select_fusion.2 = bf16[64,2,32,2048]{3,2,1,0:T(8,128)(2,1)} fusion(bf16[64,2,32,2048]{3,2,1,0:T(8,128)(2,1)} %bitcast.57, pred[64,2,32]{2,1,0:T(4,128)(4,1)S(1)} %copy.23), kind=kLoop, calls=%fused_computation.20 | loop fusion | flops 8388608 | bytes 33558528 | tf_op jit(solution)/shard_map/jit(_take)/select_n | solution.py:25
  107.5 213.7 %while.24 = (s32[]{:T(128)}, u32[2,1024]{1,0:T(2,128)S(1)}, u32[2,1024]{1,0:T(2,128)S(1)}, s32[2,2048]{1,0:T(2,128)S(1)}, s32[]{:T(128)}, /*index=5*/s32[]{:T(128)}) while((s32[]{:T(128)}, u32[2,1024]{1,0:T(2,128)S(1)}, u32[2,1024]{1,0:T(2,128)S(1)}, s32[2,2048]{1,0:T(2,128)S(1)}, s32[]{:T(128)}, /*index=5*/s32[]{:T(128)}) %tuple.40), condition=%wide.region_5.6_spmd.clone, body=%wide.region_4.5_spmd.clone.sunk | while | flops 37891 | bytes 139344 | solution.py:30
  107.5 17.7 %gather_fusion = s32[2048]{0:T(1024)S(1)} fusion(s32[2,2048]{1,0:T(2,128)S(1)} %get-tuple-element.157, u32[2048]{0:T(1024)S(1)} %bitcast.54), kind=kCustom, calls=%fused_computation.clone.clone.1 | custom fusion | bytes 32768 | tf_op jit(solution)/shard_map/vmap(jit(searchsorted))/vmap(jit(_searchsorted_scan_impl))/while/body/eval_jaxpr/gather | solution.py:30
  125.3 17.7 %gather_fusion = s32[2048]{0:T(1024)S(1)} fusion(s32[2,2048]{1,0:T(2,128)S(1)} %get-tuple-element.157, u32[2048]{0:T(1024)S(1)} %bitcast.54), kind=kCustom, calls=%fused_computation.clone.clone.1 | custom fusion | bytes 32768 | tf_op jit(solution)/shard_map/vmap(jit(searchsorted))/vmap(jit(_searchsorted_scan_impl))/while/body/eval_jaxpr/gather | solution.py:30
  143.1 17.7 %gather_fusion = s32[2048]{0:T(1024)S(1)} fusion(s32[2,2048]{1,0:T(2,128)S(1)} %get-tuple-element.157, u32[2048]{0:T(1024)S(1)} %bitcast.54), kind=kCustom, calls=%fused_computation.clone.clone.1 | custom fusion | bytes 32768 | tf_op jit(solution)/shard_map/vmap(jit(searchsorted))/vmap(jit(_searchsorted_scan_impl))/while/body/eval_jaxpr/gather | solution.py:30
  160.9 17.7 %gather_fusion = s32[2048]{0:T(1024)S(1)} fusion(s32[2,2048]{1,0:T(2,128)S(1)} %get-tuple-element.157, u32[2048]{0:T(1024)S(1)} %bitcast.54), kind=kCustom, calls=%fused_computation.clone.clone.1 | custom fusion | bytes 32768 | tf_op jit(solution)/shard_map/vmap(jit(searchsorted))/vmap(jit(_searchsorted_scan_impl))/while/body/eval_jaxpr/gather | solution.py:30
  178.8 17.7 %gather_fusion = s32[2048]{0:T(1024)S(1)} fusion(s32[2,2048]{1,0:T(2,128)S(1)} %get-tuple-element.157, u32[2048]{0:T(1024)S(1)} %bitcast.54), kind=kCustom, calls=%fused_computation.clone.clone.1 | custom fusion | bytes 32768 | tf_op jit(solution)/shard_map/vmap(jit(searchsorted))/vmap(jit(_searchsorted_scan_impl))/while/body/eval_jaxpr/gather | solution.py:30
  196.6 17.7 %gather_fusion = s32[2048]{0:T(1024)S(1)} fusion(s32[2,2048]{1,0:T(2,128)S(1)} %get-tuple-element.157, u32[2048]{0:T(1024)S(1)} %bitcast.54), kind=kCustom, calls=%fused_computation.clone.clone.1 | custom fusion | bytes 32768 | tf_op jit(solution)/shard_map/vmap(jit(searchsorted))/vmap(jit(_searchsorted_scan_impl))/while/body/eval_jaxpr/gather | solution.py:30
  214.4 17.7 %gather_fusion = s32[2048]{0:T(1024)S(1)} fusion(s32[2,2048]{1,0:T(2,128)S(1)} %get-tuple-element.157, u32[2048]{0:T(1024)S(1)} %bitcast.54), kind=kCustom, calls=%fused_computation.clone.clone.1 | custom fusion | bytes 32768 | tf_op jit(solution)/shard_map/vmap(jit(searchsorted))/vmap(jit(_searchsorted_scan_impl))/while/body/eval_jaxpr/gather | solution.py:30
  232.2 17.7 %gather_fusion = s32[2048]{0:T(1024)S(1)} fusion(s32[2,2048]{1,0:T(2,128)S(1)} %get-tuple-element.157, u32[2048]{0:T(1024)S(1)} %bitcast.54), kind=kCustom, calls=%fused_computation.clone.clone.1 | custom fusion | bytes 32768 | tf_op jit(solution)/shard_map/vmap(jit(searchsorted))/vmap(jit(_searchsorted_scan_impl))/while/body/eval_jaxpr/gather | solution.py:30
  250.0 17.7 %gather_fusion = s32[2048]{0:T(1024)S(1)} fusion(s32[2,2048]{1,0:T(2,128)S(1)} %get-tuple-element.157, u32[2048]{0:T(1024)S(1)} %bitcast.54), kind=kCustom, calls=%fused_computation.clone.clone.1 | custom fusion | bytes 32768 | tf_op jit(solution)/shard_map/vmap(jit(searchsorted))/vmap(jit(_searchsorted_scan_impl))/while/body/eval_jaxpr/gather | solution.py:30
  267.8 17.7 %gather_fusion = s32[2048]{0:T(1024)S(1)} fusion(s32[2,2048]{1,0:T(2,128)S(1)} %get-tuple-element.157, u32[2048]{0:T(1024)S(1)} %bitcast.54), kind=kCustom, calls=%fused_computation.clone.clone.1 | custom fusion | bytes 32768 | tf_op jit(solution)/shard_map/vmap(jit(searchsorted))/vmap(jit(_searchsorted_scan_impl))/while/body/eval_jaxpr/gather | solution.py:30
  285.6 17.7 %gather_fusion = s32[2048]{0:T(1024)S(1)} fusion(s32[2,2048]{1,0:T(2,128)S(1)} %get-tuple-element.157, u32[2048]{0:T(1024)S(1)} %bitcast.54), kind=kCustom, calls=%fused_computation.clone.clone.1 | custom fusion | bytes 32768 | tf_op jit(solution)/shard_map/vmap(jit(searchsorted))/vmap(jit(_searchsorted_scan_impl))/while/body/eval_jaxpr/gather | solution.py:30
  303.4 17.7 %gather_fusion = s32[2048]{0:T(1024)S(1)} fusion(s32[2,2048]{1,0:T(2,128)S(1)} %get-tuple-element.157, u32[2048]{0:T(1024)S(1)} %bitcast.54), kind=kCustom, calls=%fused_computation.clone.clone.1 | custom fusion | bytes 32768 | tf_op jit(solution)/shard_map/vmap(jit(searchsorted))/vmap(jit(_searchsorted_scan_impl))/while/body/eval_jaxpr/gather | solution.py:30
  321.9 43.3 %all-to-all-done.1 = bf16[64,2,32,2048]{3,2,1,0:T(8,128)(2,1)} async-done(((bf16[64,2,32,2048]{3,2,1,0:T(8,128)(2,1)}), bf16[64,2,32,2048]{3,2,1,0:T(8,128)(2,1)}, u32[]{:S(2)}, u32[]{:S(2)}) %all-to-all-start.1) | async-done | bytes 16777248 | tf_op jit(solution)/shard_map/all_to_all | solution.py:26
  365.1 24.3 %gather_fusion.2 = bf16[2048,2048]{1,0:T(8,128)(2,1)} fusion(bf16[4096,2048]{1,0:T(8,128)(2,1)} %bitcast.7, s32[2048]{0:T(1024)S(1)} %broadcast_clamp_fusion.2), kind=kCustom, calls=%fused_computation.2 | custom fusion | bytes 16785408 | tf_op jit(solution)/shard_map/jit(_take)/gather | solution.py:33
  389.4 15.3 %fusion.19 = f32[2,1024,2048]{2,1,0:T(8,128)} fusion(bf16[2,384,2048]{2,1,0:T(8,128)(2,1)S(1)} %copy-done, bf16[2,2048,384]{2,1,0:T(8,128)(2,1)} %param.8, bf16[2,1024,2048]{2,1,0:T(8,128)(2,1)} %bitcast.58, pred[2,1024]{1,0:T(4,128)(4,1)S(1)} %get-tuple-element.109), kind=kOutput, calls=%fused_computation.35 | convolution fusion | flops 6453723136 | bytes 31459328 | tf_op jit(solution)/shard_map/ecf,efd->ecd/dot_general | solution.py:36
  404.7 52.0 %all-reduce.2 = bf16[2,1024,2048]{2,1,0:T(8,128)(2,1)} all-reduce(f32[2,1024,2048]{2,1,0:T(8,128)} %fusion.19), channel_id=1, replica_groups=mesh['dp'=1,'tp'=2,'ep'=64] {'tp'}, use_global_device_ids=true, to_apply=%region_6.7 | all-reduce | flops 4194304 | bytes 25165824 | tf_op jit(solution)/shard_map/psum | solution.py:37
  456.7 35.8 %gather_fusion.3 = bf16[4096,2048]{1,0:T(8,128)(2,1)} fusion(bf16[2048,2048]{1,0:T(8,128)(2,1)} %bitcast.55, s32[4096]{0:T(1024)S(1)} %broadcast_clamp_fusion), kind=kCustom, calls=%fused_computation.3 | custom fusion | bytes 33570816 | tf_op jit(solution)/shard_map/jit(_take)/gather | solution.py:40
  522.7 26.5 %gather_fusion.4 = f32[4096]{0:T(1024)S(1)} fusion(f32[128,1024]{0,1:T(8,128)S(1)} %divide_bitcast_fusion, s32[4096]{0:T(1024)S(1)} %reshape.241), kind=kCustom, calls=%fused_computation.4 | custom fusion | bytes 65536 | tf_op jit(solution)/shard_map/jit(take_along_axis)/gather | solution.py:42
  550.8 396.3 %all-reduce = f32[128]{0:T(128)S(1)} all-reduce(f32[128]{0:T(128)S(1)} %dynamic-update-slice), channel_id=2, replica_groups=mesh['dp'=1,'tp'=2,'ep'=64] {'ep'}, use_global_device_ids=true, to_apply=%add | all-reduce | flops 128 | bytes 1024
  948.2 61.3 %scatter_custom_fusion = f32[1024,2048]{1,0:T(8,128)} fusion(f32[1024,2048]{1,0:T(8,128)} %convert_element_type.33, s32[4096]{0:T(1024)S(1)} %reshape.249, bf16[4096,2048]{1,0:T(8,128)(2,1)} %bitcast.19, f32[4096]{0:T(1024)S(1)} %mul.65), kind=kCustom, calls=%fused_computation.18 | custom fusion | flops 25165824 | bytes 25182208 | tf_op jit(solution)/shard_map/scatter-add | solution.py:45
  (131 shorter events, 76.0 us)
Async XLA Ops:
  0.0 389.4 %copy-start = (bf16[2,384,2048]{2,1,0:T(8,128)(2,1)S(1)}, bf16[2,384,2048]{2,1,0:T(8,128)(2,1)}, u32[]{:S(2)}) copy-start(bf16[2,384,2048]{2,1,0:T(8,128)(2,1)} %param.9) | copy-start | bytes 9437188
  27.0 62.8 %all-to-all-start = ((f32[64,2,32]{2,1,0:T(2,128)}), f32[64,2,32]{2,1,0:T(2,128)S(1)}, u32[]{:S(2)}, u32[]{:S(2)}) async-start(f32[64,2,32]{2,1,0:T(2,128)} %bitcast.1), calls=%async_computation | async-start | bytes 131072 | tf_op jit(solution)/shard_map/all_to_all | solution.py:20
  41.4 34.3 %copy-start.3 = (s32[128,32]{1,0:T(8,128)}, s32[128,32]{1,0:T(8,128)S(1)}, u32[]{:S(2)}) copy-start(s32[128,32]{1,0:T(8,128)S(1)} %top_k.24) | copy-start | bytes 49156
  89.8 275.3 %all-to-all-start.1 = ((bf16[64,2,32,2048]{3,2,1,0:T(8,128)(2,1)}), bf16[64,2,32,2048]{3,2,1,0:T(8,128)(2,1)}, u32[]{:S(2)}, u32[]{:S(2)}) async-start(bf16[64,2,32,2048]{3,2,1,0:T(8,128)(2,1)} %broadcast_select_fusion.2), calls=%async_computation.1 | async-start | bytes 33554432 | tf_op jit(solution)/shard_map/all_to_all | solution.py:26
  506.6 7.6 copy-start.4
  506.6 441.6 %all-to-all-start.2 = ((bf16[64,2,32,2048]{3,2,1,0:T(8,128)(2,1)}), bf16[64,2,32,2048]{3,2,1,0:T(8,128)(2,1)}, u32[]{:S(2)}, u32[]{:S(2)}) async-start(bf16[64,2,32,2048]{3,2,1,0:T(8,128)(2,1)} %broadcast_select_fusion.3), calls=%async_computation.2 | async-start | bytes 33554432 | tf_op jit(solution)/shard_map/all_to_all | solution.py:41
  514.2 7.6 copy-start.2
  522.7 26.6 %copy-start.5 = (u32[128]{0:T(128)S(1)}, u32[128]{0:T(128)}, u32[]{:S(2)}) copy-start(u32[128]{0:T(128)} %constant.181) | copy-start | bytes 1540
  948.2 67.4 %copy-start.1 = (bf16[2,384,2048]{2,1,0:T(8,128)(2,1)S(1)}, bf16[2,384,2048]{2,1,0:T(8,128)(2,1)}, u32[]{:S(2)}) copy-start(bf16[2,384,2048]{2,1,0:T(8,128)(2,1)} %param.9) | copy-start | bytes 9437188
where the time goes:
time: 1020 us
  blocking collectives  448 us (44%)
  local copies, waits for them, and re-layouts  343 us (34%)
  other arithmetic  135 us (13%)
  waiting for transfers between devices  43.3 us (4%)
  starting transfers between devices  29.6 us (3%)
  matrix products  15.3 us (2%)
    unnamed x1, blocking collectives  396 us
    gather x12, local copies, waits for them, and re-layouts, local_layer(): jnp.searchsorted(run_row, targets)  212 us
    scatter-add x1, other arithmetic, local_layer(): jax.ops.segment_sum(contrib.reshape(-1, d_model), cand_idx.reshape(-1), n...  61.3 us
    psum x1, blocking collectives, local_layer(): expert_out = lax.psum(part_out, 'tp').astype(jnp.bfloat16)  52 us
    all_to_all x1, waiting for transfers between devices, local_layer(): recv_rows = lax.all_to_all(send_rows, 'ep', 0, 0, tiled=True)  43.3 us
    gather x1, local copies, waits for them, and re-layouts, local_layer(): jnp.take(expert_out.reshape(-1, d_model), back_idx.reshape(-1), axis=0)  35.8 us
    gather x1, local copies, waits for them, and re-layouts, local_layer(): jnp.take(x_local, cand_idx.reshape(-1), axis=0)  34.1 us
    gather x3, local copies, waits for them, and re-layouts, local_layer(): gate_sel = jnp.take_along_axis(gate_all.T, cand_idx, axis=1)  26.7 us
  transfers between devices with their start and end apart: 3, of which 1 were waited for; matrix products, arithmetic and copies ran while one was open for 30% of the time, Pallas kernels for 0%

commit v1 on v0

v1 whole, which is shorter than its diff:
```python
import functools

import jax
import jax.numpy as jnp
import numpy as np
from jax import lax
from jax.experimental import pallas as pl
from jax.experimental.pallas import tpu as pltpu
from jax.sharding import PartitionSpec as P

CAP_FACTOR = 2
MESH = pl.DeviceIdType.MESH
SIDE = 4
WINDOW = 8
VMEM_LIMIT = 60 * 1024 * 1024


def neg(off):
    return tuple((-v) % SIDE for v in off)


def exchange_order():
    rest = [(a, b, c) for a in range(SIDE) for b in range(SIDE) for c in range(SIDE) if a or b or c]
    load = np.zeros(6)
    out = []

    def links(off):
        vec = np.zeros(6)
        for d, v in enumerate(off):
            if v in (1, 2):
                vec[2 * d] = 1
            if v in (2, 3):
                vec[2 * d + 1] = 1
        return vec

    while rest:
        best = min(rest, key=lambda o: (np.max(load + links(o)), np.sum((load + links(o)) ** 2) / (1 + links(o).sum())))
        rest.remove(best)
        out.append(best)
        load = (load + links(best)) * 0.8
    return out


ORDER = exchange_order()


def peer_of(me, core, off):
    pos = (me // (SIDE * SIDE), (me // SIDE) % SIDE, me % SIDE)
    z, y, x = (lax.rem(p + o + core * (2 * SIDE - 2 * o), SIDE) for p, o in zip(pos, off))
    return (z * SIDE + y) * SIDE + x


def route_kernel(n_cand, logit_ref, val_ref, idx_ref, gate_ref, work, soft):
    n_tok, lanes = logit_ref.shape
    step = 64
    best = jnp.full((8, lanes), -jnp.inf, jnp.float32)
    for lo in range(0, n_tok, step):
        v = logit_ref[lo:lo + step, :]
        e = jnp.exp(v - jnp.max(v, axis=1, keepdims=True))
        soft[lo:lo + step, :] = e / jnp.sum(e, axis=1, keepdims=True)
        work[lo:lo + step, :] = v
        best = jnp.maximum(best, jnp.max(v.reshape(step // 8, 8, lanes), axis=0))
    row = lax.broadcasted_iota(jnp.int32, (step, lanes), 0).astype(jnp.float32)

    def body(k, best):
        top = jnp.max(best, axis=0, keepdims=True)
        nxt = jnp.full((8, lanes), -jnp.inf, jnp.float32)
        pos = jnp.zeros((8, lanes), jnp.float32)
        gat = jnp.zeros((8, lanes), jnp.float32)
        for lo in range(0, n_tok, step):
            v = work[lo:lo + step, :]
            hit = v == top
            v = jnp.where(hit, -jnp.inf, v)
            work[lo:lo + step, :] = v
            nxt = jnp.maximum(nxt, jnp.max(v.reshape(step // 8, 8, lanes), axis=0))
            pos = pos + jnp.sum(jnp.where(hit, row + float(lo), 0.0).reshape(step // 8, 8, lanes), axis=0)
            gat = gat + jnp.sum(jnp.where(hit, soft[lo:lo + step, :], 0.0).reshape(step // 8, 8, lanes), axis=0)
        val_ref[pl.ds(k, 1), :] = top
        idx_ref[pl.ds(k, 1), :] = jnp.sum(pos, axis=0, keepdims=True).astype(jnp.int32)
        gate_ref[pl.ds(k, 1), :] = jnp.sum(gat, axis=0, keepdims=True)
        return nxt

    lax.fori_loop(0, n_cand, body, best)


def pick_kernel(idx_ref, x_ref, out_ref):
    rows = idx_ref.shape[0]
    n_tok = x_ref.shape[0]
    onehot = (lax.broadcasted_iota(jnp.int32, (rows, n_tok), 1) == idx_ref[...]).astype(jnp.bfloat16)
    out_ref[...] = jnp.dot(onehot, x_ref[...], preferred_element_type=jnp.float32).astype(jnp.bfloat16)


def run_window(copies):
    for j, c in enumerate(copies):
        if j >= WINDOW:
            copies[j - WINDOW].wait()
        c.start()
    for c in copies[-WINDOW:]:
        c.wait()


def dispatch_kernel(rows_ref, val_ref, wu_ref, wd_ref, rrows_ref, rval_ref, wup_ref, wdp_ref, send, recv, vsend, vrecv, wsend, wrecv, loc):
    me, core = lax.axis_index("ep"), lax.axis_index("tp")
    other = 1 - core
    weights = [
        pltpu.make_async_remote_copy(src.at[other], dst, wsend.at[i], wrecv.at[i], device_id={"tp": other}, device_id_type=MESH)
        for i, (src, dst) in enumerate(((wu_ref, wup_ref), (wd_ref, wdp_ref)))
    ]
    own = [pltpu.make_async_copy(rows_ref.at[me], rrows_ref.at[me], loc.at[0]), pltpu.make_async_copy(val_ref.at[me], rval_ref.at[me], loc.at[1])]
    copies, vals = [], []
    for j, off in enumerate(ORDER):
        to = peer_of(me, core, off)
        copies.append(pltpu.make_async_remote_copy(rows_ref.at[to], rrows_ref.at[me], send.at[j], recv.at[j], device_id={"ep": to}, device_id_type=MESH))
        vals.append(pltpu.make_async_remote_copy(val_ref.at[to], rval_ref.at[me], vsend.at[j], vrecv.at[j], device_id={"ep": to}, device_id_type=MESH))
    for c in own + weights + vals:
        c.start()
    run_window(copies)
    for c in own + weights + vals:
        c.wait()


def expert_kernel(capacity, core_ref, vcol_ref, vrow_ref, x_ref, wu_ref, wup_ref, wd_ref, wdp_ref, out_ref):
    x = x_ref[...]
    above = (vrow_ref[...] > vcol_ref[...]).astype(jnp.float32)
    keep = jnp.sum(above, axis=1, keepdims=True) < float(capacity)
    z = None
    for up, down in ((wu_ref[0], wd_ref[0]), (wup_ref[...], wdp_ref[...])):
        pre = jnp.dot(x, up, preferred_element_type=jnp.float32)
        hid = jax.nn.gelu(pre, approximate=True).astype(jnp.bfloat16)
        part = jnp.dot(hid, down, preferred_element_type=jnp.float32)
        z = part if z is None else z + part
    out_ref[...] = jnp.where(keep, z, 0.0).astype(jnp.bfloat16)


def return_kernel(z_ref, ret_ref, send, recv, loc):
    me, core = lax.axis_index("ep"), lax.axis_index("tp")
    half = z_ref.shape[2] // 2
    part = [z_ref.at[:, :, pl.ds(pl.multiple_of(h * half, half), half)] for h in (core, 1 - core)]
    own = pltpu.make_async_copy(part[0].at[me], ret_ref.at[me, core], loc)
    copies = [pltpu.make_async_remote_copy(part[1].at[me], ret_ref.at[me, core], send.at[0], recv.at[0], device_id={"tp": 1 - core}, device_id_type=MESH)]
    for j, off in enumerate(ORDER):
        to = peer_of(me, core, off)
        for h in range(2):
            sem = 1 + 2 * j + h
            copies.append(pltpu.make_async_remote_copy(part[h].at[to], ret_ref.at[me, core], send.at[sem], recv.at[sem], device_id={"tp": (core + h) % 2, "ep": to}, device_id_type=MESH))
    own.start()
    for j, c in enumerate(copies):
        if j >= 2 * WINDOW:
            copies[j - 2 * WINDOW].wait()
        c.start()
    for c in copies[-2 * WINDOW:]:
        c.wait()
    own.wait()


def combine_kernel(core_ref, idx_ref, gate_ref, z_ref, x_ref, out_ref, acc):
    step = pl.program_id(0)
    n_tok = x_ref.shape[0]
    rows = z_ref.shape[0]
    hit = lax.broadcasted_iota(jnp.int32, (n_tok, rows), 0) == idx_ref[...]
    left = gate_ref[...]
    total = None
    z = z_ref[...]
    for _ in range(3):
        piece = left.astype(jnp.bfloat16)
        left = left - piece.astype(jnp.float32)
        mat = jnp.where(hit, piece.astype(jnp.float32), 0.0).astype(jnp.bfloat16)
        part = jnp.dot(mat, z, preferred_element_type=jnp.float32)
        total = part if total is None else total + part

    @pl.when(step == 0)
    def _():
        acc[...] = total

    @pl.when(step > 0)
    def _():
        acc[...] += total

    @pl.when(step == pl.num_programs(0) - 1)
    def _():
        out_ref[...] = (x_ref[...].astype(jnp.float32) + acc[...]).astype(jnp.bfloat16)


def solution(mesh):
    n_groups = mesh.shape["ep"]
    any_spec = pl.BlockSpec(memory_space=pl.ANY)
    dma = pltpu.SemaphoreType.DMA
    n_off = len(ORDER)
    side_effects = pltpu.CompilerParams(has_side_effects=True)

    def local_layer(x_local, logit_local, w_up, w_down):
        n_tok, d_model = x_local.shape
        n_experts = logit_local.shape[1]
        own_experts, _, hid = w_up.shape
        capacity = CAP_FACTOR * n_tok * n_groups // n_experts
        cand = 2 * capacity // n_groups
        rows = n_groups * cand
        half = d_model // 2
        core = lax.axis_index("tp")
        core_arr = core.reshape(1).astype(jnp.int32)

        small = lambda dt: jax.ShapeDtypeStruct((cand, n_experts), dt)
        val, idx, gate = pl.pallas_call(
            functools.partial(route_kernel, cand),
            out_shape=(small(jnp.float32), small(jnp.int32), small(jnp.float32)),
            scratch_shapes=[pltpu.VMEM((n_tok, n_experts), jnp.float32), pltpu.VMEM((n_tok, n_experts), jnp.float32)],
        )(logit_local)
        mine = lambda a: lax.dynamic_index_in_dim(a.T.reshape(n_groups, own_experts, cand), core, 1, keepdims=False)
        val_send = jnp.pad(mine(val), ((0, 0), (0, 128 - cand))).reshape(n_groups, 1, 128)
        pick_idx = mine(idx).reshape(rows, 1)

        blk = 256
        send_rows = pl.pallas_call(
            pick_kernel,
            out_shape=jax.ShapeDtypeStruct((rows, d_model), jnp.bfloat16),
            grid=(rows // blk,),
            in_specs=[pl.BlockSpec((blk, 1), lambda i: (i, 0)), pl.BlockSpec((n_tok, d_model), lambda i: (0, 0))],
            out_specs=pl.BlockSpec((blk, d_model), lambda i: (i, 0)),
            compiler_params=pltpu.CompilerParams(vmem_limit_bytes=VMEM_LIMIT),
        )(pick_idx, x_local).reshape(n_groups, cand, d_model)

        recv_rows, recv_val, wu_peer, wd_peer = pl.pallas_call(
            dispatch_kernel,
            out_shape=(
                jax.ShapeDtypeStruct((n_groups, cand, d_model), jnp.bfloat16),
                jax.ShapeDtypeStruct((n_groups, 1, 128), jnp.float32),
                jax.ShapeDtypeStruct(w_up.shape[1:], jnp.bfloat16),
                jax.ShapeDtypeStruct(w_down.shape[1:], jnp.bfloat16),
            ),
            in_specs=[any_spec] * 4,
            out_specs=(any_spec,) * 4,
            scratch_shapes=[dma((n_off,)), dma((n_off,)), dma((n_off,)), dma((n_off,)), dma((2,)), dma((2,)), dma((2,))],
            compiler_params=side_effects,
        )(send_rows, val_send, w_up, w_down)

        cand_val = recv_val[:, 0, :cand].reshape(rows)
        z = pl.pallas_call(
            functools.partial(expert_kernel, capacity),
            out_shape=jax.ShapeDtypeStruct((rows, d_model), jnp.bfloat16),
            grid_spec=pltpu.PrefetchScalarGridSpec(
                num_scalar_prefetch=1,
                grid=(rows // blk,),
                in_specs=[
                    pl.BlockSpec((blk, 1), lambda i, c: (i, 0)),
                    pl.BlockSpec((1, rows), lambda i, c: (0, 0)),
                    pl.BlockSpec((blk, d_model), lambda i, c: (i, 0)),
                    pl.BlockSpec((1, d_model, hid), lambda i, c: (c[0], 0, 0)),
                    pl.BlockSpec((d_model, hid), lambda i, c: (0, 0)),
                    pl.BlockSpec((1, hid, d_model), lambda i, c: (c[0], 0, 0)),
                    pl.BlockSpec((hid, d_model), lambda i, c: (0, 0)),
                ],
                out_specs=pl.BlockSpec((blk, d_model), lambda i, c: (i, 0)),
            ),
            compiler_params=pltpu.CompilerParams(vmem_limit_bytes=VMEM_LIMIT),
        )(core_arr, cand_val.reshape(rows, 1), cand_val.reshape(1, rows), recv_rows.reshape(rows, d_model), w_up, wu_peer, w_down, wd_peer)

        ret = pl.pallas_call(
            return_kernel,
            out_shape=jax.ShapeDtypeStruct((n_groups, own_experts, cand, half), jnp.bfloat16),
            in_specs=[any_spec],
            out_specs=any_spec,
            scratch_shapes=[dma((2 * n_off + 1,)), dma((2 * n_off + 1,)), dma],
            compiler_params=side_effects,
        )(z.reshape(n_groups, cand, d_model))

        slots = n_experts * cand
        kblk = 512
        out_half = pl.pallas_call(
            combine_kernel,
            out_shape=jax.ShapeDtypeStruct((n_tok, half), jnp.bfloat16),
            grid_spec=pltpu.PrefetchScalarGridSpec(
                num_scalar_prefetch=1,
                grid=(slots // kblk,),
                in_specs=[
                    pl.BlockSpec((1, kblk), lambda i, c: (0, i)),
                    pl.BlockSpec((1, kblk), lambda i, c: (0, i)),
                    pl.BlockSpec((kblk, half), lambda i, c: (i, 0)),
                    pl.BlockSpec((n_tok, half), lambda i, c: (0, c[0])),
                ],
                out_specs=pl.BlockSpec((n_tok, half), lambda i, c: (0, 0)),
                scratch_shapes=[pltpu.VMEM((n_tok, half), jnp.float32)],
            ),
            compiler_params=pltpu.CompilerParams(vmem_limit_bytes=VMEM_LIMIT),
        )(core_arr, idx.T.reshape(1, slots), gate.T.reshape(1, slots), ret.reshape(slots, half), x_local)
        return lax.all_gather(out_half, "tp", axis=1, tiled=True)

    token_spec = P(("dp", "ep"), None)
    return jax.shard_map(local_layer, mesh=mesh, in_specs=(token_spec, token_spec, P("ep", None, "tp"), P("ep", "tp", None)), out_specs=token_spec, check_vma=False)
```

time: 1020 us -> 391 us (0.38)
  the two profiles are of different devices: /device:TPU:2 before, /device:TPU:1 now
where the time goes in v1:
time: 391 us
  Pallas kernels  341 us (87%)
  waiting for transfers between devices  22 us (6%)
  local copies, waits for them, and re-layouts  15 us (4%)
  between operations  13.4 us (3%)
    pallas_call x1, Pallas kernels, local_layer(): pl.pallas_call(dispatch_kernel, out_shape=(jax.ShapeDtypeStruct((n_groups...  134 us
    pallas_call x1, Pallas kernels, local_layer(): pl.pallas_call(return_kernel, out_shape=jax.ShapeDtypeStruct((n_groups, o...  126 us
    pallas_call x1, Pallas kernels, local_layer(): pl.pallas_call(combine_kernel, out_shape=jax.ShapeDtypeStruct((n_tok, hal...  34.4 us
    pallas_call x1, Pallas kernels, local_layer(): pl.pallas_call(functools.partial(expert_kernel, capacity), out_shape=jax....  24.9 us
    all_gather x1, waiting for transfers between devices, local_layer(): return lax.all_gather(out_half, 'tp', axis=1, tiled=True)  22 us
    pallas_call x1, Pallas kernels, local_layer(): pl.pallas_call(pick_kernel, out_shape=jax.ShapeDtypeStruct((rows, d_model...  14.1 us
  transfers between devices with their start and end apart: 1, of which 1 were waited for; matrix products, arithmetic and copies ran while one was open for 0% of the time, Pallas kernels for 0%

profile of v1, /device:TPU:1, one launch (start us, length us, event | category | flops | bytes accessed | tf_op | source)
XLA Modules:
  0.0 391.0 jit_solution(7872631573807723744)
XLA Ops:
  6.5 0.0 all-gather.2.cloned.1.call-start
  6.5 7.2 %shard_map.46 = (f32[32,128]{1,0:T(8,128)}, s32[32,128]{1,0:T(8,128)}, f32[32,128]{1,0:T(8,128)}) custom-call(f32[1024,128]{1,0:T(8,128)} %logit_ref.1), custom_call_target="tpu_custom_call" | custom-call | tf_op jit(solution)/shard_map/pallas_call | solution.py:203
  13.8 0.8 copy.9
  14.6 0.7 reshape.35.idx_ref
  15.3 0.8 copy.10
  16.1 0.7 reshape.36.gate_ref
  16.8 0.8 copy.13
  17.6 0.1 dynamic-slice_reduce_fusion
  17.7 2.1 reshape.45.idx_ref
  19.8 0.6 pad.4
  20.4 14.1 %shard_map.47 = bf16[2048,2048]{1,0:T(8,128)(2,1)} custom-call(s32[2048,1]{1,0:T(8,128)} %reshape.45.idx_ref, bf16[1024,2048]{1,0:T(8,128)(2,1)} %x_ref.3), custom_call_target="tpu_custom_call" | custom-call | tf_op jit(solution)/shard_map/pallas_call | solution.py:213
  34.5 133.9 %shard_map.48 = (bf16[64,32,2048]{2,1,0:T(8,128)(2,1)}, f32[64,1,128]{2,1,0:T(1,128)}, bf16[2048,384]{1,0:T(8,128)(2,1)}, bf16[384,2048]{1,0:T(8,128)(2,1)}) custom-call(bf16[64,32,2048]{2,1,0:T(8,128)(2,1)} %bitcast.13, f32[64,1,128]{2,1,0:T(1,128)} %bitcast.19, bf16[2,2048,384]{2,1,0:T(8,128)(2,1)} %wu_ref.3, bf16[2,384,2048]{2,1,0:T(8,128)(2,1)} %wd_ref.3), custom_call_target="tpu_custom_call" | custom-call | tf_op jit(solution)/shard_map/pallas_call | solution.py:222
  168.4 0.9 fusion
  169.2 0.7 reshape_reshape_squeeze.7.vrow_ref
  169.9 2.0 reshape_reshape_squeeze.8.vcol_ref
  172.0 24.9 %shard_map.49 = bf16[2048,2048]{1,0:T(8,128)(2,1)} custom-call(s32[1]{0:T(128)} %bitcast.core_ref, f32[2048,1]{1,0:T(8,128)} %reshape_reshape_squeeze.8.vcol_ref, f32[1,2048]{1,0:T(1,128)} %reshape_reshape_squeeze.7.vrow_ref, bf16[2048,2048]{1,0:T(8,128)(2,1)} %bitcast.16, bf16[2,2048,384]{2,1,0:T(8,128)(2,1)} %wu_ref.3, ...), custom_call_target="tpu_custom_call" | custom-call | tf_op jit(solution)/shard_map/pallas_call | solution.py:237
  196.9 126.1 %shard_map.50 = bf16[64,2,32,1024]{3,2,1,0:T(8,128)(2,1)} custom-call(bf16[64,32,2048]{2,1,0:T(8,128)(2,1)} %bitcast.15), custom_call_target="tpu_custom_call" | custom-call | tf_op jit(solution)/shard_map/pallas_call | solution.py:257
  323.0 34.4 %shard_map.51 = bf16[1024,1024]{1,0:T(8,128)(2,1)} custom-call(s32[1]{0:T(128)} %bitcast.core_ref, s32[1,4096]{1,0:T(1,128)} %reshape.35.idx_ref, f32[1,4096]{1,0:T(1,128)} %reshape.36.gate_ref, bf16[4096,1024]{1,0:T(8,128)(2,1)} %bitcast.14, bf16[1024,2048]{1,0:T(8,128)(2,1)} %x_ref.3), custom_call_target="tpu_custom_call" | custom-call | tf_op jit(solution)/shard_map/pallas_call | solution.py:268
  357.4 0.0 all-gather.2.cloned.1.call-update
  357.4 22.0 %all-gather.2.cloned.1.call-done = bf16[1024,2048]{1,0:T(8,128)(2,1)} async-done(((bf16[1024,1024]{1,0:T(8,128)(2,1)}), bf16[1024,2048]{1,0:T(8,128)(2,1)}) %all-gather.2.cloned.1.call-update) | async-done | bytes 4194320 | tf_op jit(solution)/shard_map/all_gather | solution.py:285
  379.4 4.8 %copy.16 = bf16[1024,2048]{1,0:T(8,128)(2,1)} copy(bf16[1024,2048]{1,0:T(8,128)(2,1)} %all-gather.2.cloned.1.call-done) | data formatting | bytes 8388608
  (1 shorter events, 0.0 us)
Async XLA Ops:
  6.5 372.8 %all-gather.2.cloned.1.call-start = ((), (), s32[]{:S(2)}) async-start(), calls=%async_computation | async-start | bytes 6291456 | tf_op jit(solution)/shard_map/all_gather | solution.py:285
Sparse Core Ops, SparseCore 0:
  357.5 21.7 all-gather.1

commit v2 on v0

v2 whole, which is shorter than its diff:
```python
import functools

import jax
import jax.numpy as jnp
from jax import lax
from jax.experimental import pallas as pl
from jax.experimental.pallas import tpu as pltpu
from jax.sharding import PartitionSpec as P

CAP_FACTOR = 2
MESH = pl.DeviceIdType.MESH
SIDE = 4
LAG = 2.0
EARLY = 2.0
AHEAD = 4.0
VMEM_LIMIT = 62 * 1024 * 1024
SELF = (0, 0, 0)


def neg(off):
    return tuple((-v) % SIDE for v in off)


def plan(lag):
    jobs = [(a, b, c) for a in range(SIDE) for b in range(SIDE) for c in range(SIDE) if a or b or c]
    dur = {1: 1.0, 3: 1.0, 2: 2.0}
    rem = {o: {d for d in range(3) if o[d]} for o in jobs}
    ready = {o: 0.0 for o in jobs}
    count = {o: 0 for o in jobs}
    free = [0.0] * 3
    legs = []
    while any(rem.values()):
        d = min((d for d in range(3) if any(d in rem[o] for o in jobs)), key=lambda d: free[d])
        cand = [o for o in jobs if d in rem[o]]
        avail = [o for o in cand if ready[o] <= free[d] + 1e-9]
        if not avail:
            free[d] = min(ready[o] for o in cand)
            continue
        o = min(avail, key=lambda o: (-len(rem[o]), -sum(dur[o[q]] for q in rem[o]), sum(o[q] * (7, 3, 5)[q] for q in range(3)) % 11, o))
        rem[o].discard(d)
        legs.append((free[d], o, d, count[o]))
        count[o] += 1
        free[d] += dur[o[d]]
        ready[o] = free[d] + lag
    return sorted(legs), {o: ready[o] - lag for o in jobs}, count


LEGS, FINISH, N_LEGS = plan(LAG)
START = {o: t for t, o, _, i in LEGS if i == 0}
LEG_ID = {(o, i): k for k, (_, o, _, i) in enumerate(LEGS)}
JOB_ID = {o: j for j, o in enumerate(sorted(FINISH))}
SEND_ORDER = sorted(FINISH, key=lambda o: (START[o], o)) + [SELF]
DONE_ORDER = [SELF] + sorted(FINISH, key=lambda o: (FINISH[o], o))
SEND_SLOT = {o: p for p, o in enumerate(SEND_ORDER)}
DONE_SLOT = {o: r for r, o in enumerate(DONE_ORDER)}
FINISH_ALL = {SELF: 0.0, **FINISH}


def peer_at(me, core, off):
    pos = (me // (SIDE * SIDE), (me // SIDE) % SIDE, me % SIDE)
    z, y, x = (lax.rem(p + o + core * (2 * SIDE - 2 * o), SIDE) for p, o in zip(pos, off))
    return (z * SIDE + y) * SIDE + x


def leg_peer(me, core, off, axis):
    return peer_at(me, core, tuple(v if q == axis else 0 for q, v in enumerate(off)))


def leg_time(leg):
    t, _, _, i = leg
    return t - (EARLY if i == 0 else 0.0)


def group_events(compute_times):
    groups, rest = [], sorted(LEGS, key=lambda leg: (leg_time(leg), leg))
    for t in compute_times:
        groups.append([leg for leg in rest if leg_time(leg) < t])
        rest = [leg for leg in rest if leg_time(leg) >= t]
    return groups + [rest]


def lane_column(table, lane):
    lanes = lax.broadcasted_iota(jnp.int32, table.shape, 1)
    return jnp.sum(jnp.where(lanes == lane, table, 0.0), axis=1, keepdims=True)


def route_kernel(n_cand, logit_ref, val_ref, idx_ref, gate_ref, work, soft):
    n_tok, lanes = logit_ref.shape
    step = 64
    best = jnp.full((8, lanes), -jnp.inf, jnp.float32)
    for lo in range(0, n_tok, step):
        v = logit_ref[lo:lo + step, :]
        e = jnp.exp(v - jnp.max(v, axis=1, keepdims=True))
        soft[lo:lo + step, :] = e / jnp.sum(e, axis=1, keepdims=True)
        work[lo:lo + step, :] = v
        best = jnp.maximum(best, jnp.max(v.reshape(step // 8, 8, lanes), axis=0))
    row = lax.broadcasted_iota(jnp.int32, (step, lanes), 0).astype(jnp.float32)

    def body(k, best):
        top = jnp.max(best, axis=0, keepdims=True)
        nxt = jnp.full((8, lanes), -jnp.inf, jnp.float32)
        pos = jnp.zeros((8, lanes), jnp.float32)
        gat = jnp.zeros((8, lanes), jnp.float32)
        for lo in range(0, n_tok, step):
            v = work[lo:lo + step, :]
            hit = v == top
            v = jnp.where(hit, -jnp.inf, v)
            work[lo:lo + step, :] = v
            nxt = jnp.maximum(nxt, jnp.max(v.reshape(step // 8, 8, lanes), axis=0))
            pos = pos + jnp.sum(jnp.where(hit, row + float(lo), 0.0).reshape(step // 8, 8, lanes), axis=0)
            gat = gat + jnp.sum(jnp.where(hit, soft[lo:lo + step, :], 0.0).reshape(step // 8, 8, lanes), axis=0)
        val_ref[pl.ds(k, 1), :] = top
        idx_ref[pl.ds(k, 1), :] = jnp.sum(pos, axis=0, keepdims=True)
        gate_ref[pl.ds(k, 1), :] = jnp.sum(gat, axis=0, keepdims=True)
        return nxt

    lax.fori_loop(0, n_cand, body, best)


def expert_kernel(capacity, idx_ref, x_ref, val_ref, wu_ref, wd_ref, z_ref,
                  cols, outbox, hop1, hop2, inbox, rval, wu, wd, zbuf, send, recv, vsend, vrecv, wsend, wrecv, lsem, zsem):
    me, core = lax.axis_index("ep"), lax.axis_index("tp")
    other = 1 - core
    n_slot, cand, d_model = outbox.shape
    n_tok, lanes = x_ref.shape[0], val_ref.shape[2]
    per = 8
    rows = per * cand
    n_chunk = n_slot // per
    hops = (hop1, hop2)
    own_experts = wu_ref.shape[0]

    weights = []
    for i, (src, dst) in enumerate(((wu_ref, wu), (wd_ref, wd))):
        weights.append(pltpu.make_async_copy(src.at[core], dst.at[0], lsem.at[i]))
        weights.append(pltpu.make_async_remote_copy(src.at[other], dst.at[1], wsend.at[i], wrecv.at[i], device_id={"tp": other}, device_id_type=MESH))
    own_val = pltpu.make_async_copy(val_ref.at[own_experts * me + core], rval.at[DONE_SLOT[SELF]], lsem.at[2])

    def val_copy(o):
        to = peer_at(me, core, o)
        j = JOB_ID[o]
        return pltpu.make_async_remote_copy(val_ref.at[own_experts * to + core], rval.at[DONE_SLOT[o]], vsend.at[j], vrecv.at[j], device_id={"ep": to}, device_id_type=MESH)

    def leg_copy(o, axis, i):
        last = i == N_LEGS[o] - 1
        src = outbox.at[SEND_SLOT[o]] if i == 0 else hops[i - 1].at[JOB_ID[o]]
        dst = inbox.at[DONE_SLOT[o]] if last else hops[i].at[JOB_ID[o]]
        k = LEG_ID[o, i]
        return pltpu.make_async_remote_copy(src, dst, send.at[k], recv.at[k], device_id={"ep": leg_peer(me, core, o, axis)}, device_id_type=MESH)

    def arrival(o, i):
        return pltpu.make_async_remote_copy(inbox.at[0], inbox.at[0], send.at[0], recv.at[LEG_ID[o, i]], device_id={"tp": other}, device_id_type=MESH)

    def run_legs(legs):
        for _, o, axis, i in legs:
            if i:
                arrival(o, i - 1).wait_recv()
            leg_copy(o, axis, i).start()

    idx = idx_ref[...]

    def set_columns(p):
        o = SEND_ORDER[p]
        cols[p * cand:(p + 1) * cand, :] = lane_column(idx, own_experts * peer_at(me, core, o) + core)

    pick_times = [min(leg_time((START[o], o, 0, 0)) for o in SEND_ORDER[g * per:(g + 1) * per] if o != SELF) - AHEAD for g in range(n_chunk)]
    done_times = [max(FINISH_ALL[o] for o in DONE_ORDER[g * per:(g + 1) * per]) + LAG for g in range(n_chunk)]
    groups = group_events(pick_times + done_times)

    for p in range(per):
        set_columns(p)

    def pick(g, c):
        for k in range(n_chunk):
            @pl.when(g == k)
            def _():
                run_legs(groups[k])
        at = pl.multiple_of(g * rows, rows)
        onehot = (lax.broadcasted_iota(jnp.int32, (rows, n_tok), 1).astype(jnp.float32) == cols[pl.ds(at, rows), :]).astype(jnp.bfloat16)
        got = jnp.dot(onehot, x_ref[...], preferred_element_type=jnp.float32).astype(jnp.bfloat16)
        outbox[pl.ds(g * per, per)] = got.reshape(per, cand, d_model)

        @pl.when(g == 0)
        def _():
            for c in weights + [own_val]:
                c.start()
            for o in FINISH:
                val_copy(o).start()
            for p in range(per, n_slot):
                set_columns(p)
        return c

    lax.fori_loop(0, n_chunk, pick, 0)
    inbox[DONE_SLOT[SELF]] = outbox[SEND_SLOT[SELF]]

    def expert(g, c):
        for k in range(n_chunk):
            @pl.when(g == k)
            def _():
                run_legs(groups[n_chunk + k])
                if k == 0:
                    for o in FINISH:
                        val_copy(o).wait_recv()
                    for c in weights + [own_val]:
                        c.wait()
                for o in DONE_ORDER[k * per:(k + 1) * per]:
                    if o != SELF:
                        arrival(o, N_LEGS[o] - 1).wait_recv()
                if k == n_chunk - 1:
                    run_legs(groups[2 * n_chunk])
        eye = lax.broadcasted_iota(jnp.int32, (cand, lanes), 0) == lax.broadcasted_iota(jnp.int32, (cand, lanes), 1)
        mine = jnp.concatenate([jnp.sum(jnp.where(eye, rval[g * per + i], 0.0), axis=1, keepdims=True) for i in range(per)], axis=0)
        pad = lax.broadcasted_iota(jnp.int32, (1, lanes), 1) < cand

        def count(j, acc):
            return acc + (jnp.where(pad, rval[j], -jnp.inf) > mine).astype(jnp.float32)

        above = lax.fori_loop(0, n_slot, count, jnp.zeros((rows, lanes), jnp.float32), unroll=8)
        keep = jnp.sum(above, axis=1, keepdims=True) < float(capacity)
        x = inbox[pl.ds(g * per, per)].reshape(rows, d_model)
        z = None
        for h in range(2):
            pre = jnp.dot(x, wu[h], preferred_element_type=jnp.float32)
            hid = jax.nn.gelu(pre, approximate=True).astype(jnp.bfloat16)
            part = jnp.dot(hid, wd[h], preferred_element_type=jnp.float32)
            z = part if z is None else z + part
        slot = lax.rem(g, 2)

        def flush(g, slot):
            return pltpu.make_async_copy(zbuf.at[slot], z_ref.at[pl.ds(g * per, per)], zsem.at[slot])

        @pl.when(g >= 2)
        def _():
            flush(g - 2, slot).wait()
        zbuf[slot] = jnp.where(keep, z, 0.0).astype(jnp.bfloat16).reshape(per, cand, d_model)
        flush(g, slot).start()

        @pl.when(g == n_chunk - 1)
        def _():
            flush(g - 1, 1 - slot).wait()
            flush(g, slot).wait()
        return c

    lax.fori_loop(0, n_chunk, expert, 0)

    def drain(k, c):
        pltpu.make_async_remote_copy(inbox.at[0], inbox.at[0], send.at[k], recv.at[0], device_id={"tp": other}, device_id_type=MESH).wait_send()
        return c

    lax.fori_loop(0, len(LEGS), drain, 0)

    def vdrain(k, c):
        pltpu.make_async_remote_copy(rval.at[0], rval.at[0], vsend.at[k], vrecv.at[0], device_id={"tp": other}, device_id_type=MESH).wait_send()
        return c

    lax.fori_loop(0, len(FINISH), vdrain, 0)


def combine_kernel(idx_ref, gate_ref, x_ref, z_ref, out_ref,
                   ids, gts, hop1, hop2, back, acc, xh, obuf, send, recv, asend, arecv, bsend, brecv, lsem, osend, orecv, osem):
    me, core = lax.axis_index("ep"), lax.axis_index("tp")
    other = 1 - core
    n_slot, n_par, cand, half = back.shape
    n_tok = x_ref.shape[0]
    per = 4
    rows = per * n_par * cand
    n_chunk = n_slot // per
    hops = (hop1, hop2)
    mine = pl.ds(pl.multiple_of(core * half, half), half)
    theirs = pl.ds(pl.multiple_of(other * half, half), half)

    def source(o, i):
        return z_ref.at[DONE_SLOT[neg(o)]] if i == 0 else hops[i - 1].at[JOB_ID[o]]

    def last_copies(o, src, to):
        j = DONE_SLOT[o]
        dst = back.at[j, core]
        same = None if to is None else pltpu.make_async_remote_copy(src.at[:, mine], dst, asend.at[j], arecv.at[j], device_id={"ep": to}, device_id_type=MESH)
        there = {"tp": other} if to is None else {"tp": other, "ep": to}
        cross = pltpu.make_async_remote_copy(src.at[:, theirs], dst, bsend.at[j], brecv.at[j], device_id=there, device_id_type=MESH)
        return same, cross

    def dummy(s, r):
        return pltpu.make_async_remote_copy(back.at[0, 0], back.at[0, 0], s, r, device_id={"tp": other}, device_id_type=MESH)

    def full(s, r):
        return pltpu.make_async_remote_copy(hop1.at[0], hop1.at[0], s, r, device_id={"tp": other}, device_id_type=MESH)

    def run_legs(legs):
        for _, o, axis, i in legs:
            if i:
                full(send.at[0], recv.at[LEG_ID[o, i - 1]]).wait_recv()
            to = leg_peer(me, core, o, axis)
            if i == N_LEGS[o] - 1:
                for c in last_copies(o, source(o, i), to):
                    c.start()
            else:
                k = LEG_ID[o, i]
                pltpu.make_async_remote_copy(source(o, i), hops[i].at[JOB_ID[o]], send.at[k], recv.at[k], device_id={"ep": to}, device_id_type=MESH).start()

    done_times = [max(FINISH_ALL[o] for o in DONE_ORDER[g * per:(g + 1) * per]) + LAG for g in range(n_chunk)]
    groups = group_events(done_times)

    x_copy = pltpu.make_async_copy(x_ref.at[:, mine], xh, lsem.at[0])
    own = pltpu.make_async_copy(z_ref.at[DONE_SLOT[SELF]].at[:, mine], back.at[DONE_SLOT[SELF], core], lsem.at[1])
    _, cross = last_copies(SELF, z_ref.at[DONE_SLOT[SELF]], None)
    first = [leg for leg in groups[0] if leg[3] == 0]
    run_legs(first)
    groups[0] = [leg for leg in groups[0] if leg[3] != 0]
    for c in (own, cross, x_copy):
        c.start()

    tables = ((idx_ref[...], ids), (gate_ref[...], gts))
    eye = lax.broadcasted_iota(jnp.int32, (rows, rows), 0) == lax.broadcasted_iota(jnp.int32, (rows, rows), 1)
    n_owner = idx_ref.shape[1]
    own_experts = n_par
    for g in range(n_chunk):
        lanes = []
        for o in DONE_ORDER[g * per:(g + 1) * per]:
            for p in range(n_par):
                lanes.append(own_experts * peer_at(me, p, neg(o)) + p)
        for table, rows_out in tables:
            col = jnp.concatenate([lane_column(table, e) for e in lanes], axis=0)
            rows_out[g:g + 1, :] = jnp.sum(jnp.where(eye, col, 0.0), axis=0, keepdims=True)

    def combine(g, c):
        for k in range(n_chunk):
            @pl.when(g == k)
            def _():
                run_legs(groups[k])
                if k == n_chunk - 1:
                    run_legs(groups[n_chunk])
                for o in DONE_ORDER[k * per:(k + 1) * per]:
                    j = DONE_SLOT[o]
                    if o == SELF:
                        own.wait()
                    else:
                        dummy(asend.at[j], arecv.at[j]).wait_recv()
                    dummy(bsend.at[j], brecv.at[j]).wait_recv()
        z = back[pl.ds(g * per, per)].reshape(rows, half)
        hit = lax.broadcasted_iota(jnp.int32, (n_tok, rows), 0).astype(jnp.float32) == ids[pl.ds(g, 1), :]
        left = gts[pl.ds(g, 1), :]
        total = None
        for _ in range(3):
            piece = left.astype(jnp.bfloat16)
            left = left - piece.astype(jnp.float32)
            mat = jnp.where(hit, piece.astype(jnp.float32), 0.0).astype(jnp.bfloat16)
            part = jnp.dot(mat, z, preferred_element_type=jnp.float32)
            total = part if total is None else total + part

        @pl.when(g == 0)
        def _():
            acc[...] = total

        @pl.when(g > 0)
        def _():
            acc[...] += total
        return c

    lax.fori_loop(0, n_chunk, combine, 0)
    x_copy.wait()
    n_part = osend.shape[0]
    size = n_tok // n_part

    def out_copies(b):
        at = pl.ds(pl.multiple_of(b * size, size), size)
        src, dst = obuf.at[at], out_ref.at[at, mine]
        return (pltpu.make_async_copy(src, dst, osem.at[b]),
                pltpu.make_async_remote_copy(src, dst, osend.at[b], orecv.at[b], device_id={"tp": other}, device_id_type=MESH))

    def finish(b, c):
        at = pl.ds(pl.multiple_of(b * size, size), size)
        obuf[at, :] = (xh[at, :].astype(jnp.float32) + acc[at, :]).astype(jnp.bfloat16)
        for copy in out_copies(b):
            copy.start()
        return c

    lax.fori_loop(0, n_part, finish, 0)

    def drain_out(b, c):
        for copy in out_copies(b):
            copy.wait()
        return c

    lax.fori_loop(0, n_part, drain_out, 0)
    for leg in LEGS:
        if leg[3] < N_LEGS[leg[1]] - 1:
            full(send.at[LEG_ID[leg[1], leg[3]]], recv.at[0]).wait_send()

    def drain(j, c):
        @pl.when(j != DONE_SLOT[SELF])
        def _():
            dummy(asend.at[j], arecv.at[j]).wait_send()
        dummy(bsend.at[j], brecv.at[j]).wait_send()
        return c

    lax.fori_loop(0, n_slot, drain, 0)


def solution(mesh):
    n_groups = mesh.shape["ep"]
    any_spec = pl.BlockSpec(memory_space=pl.ANY)
    vmem_spec = pl.BlockSpec(memory_space=pltpu.VMEM)
    dma = pltpu.SemaphoreType.DMA
    n_legs, n_jobs = len(LEGS), len(FINISH)
    params = pltpu.CompilerParams(has_side_effects=True, vmem_limit_bytes=VMEM_LIMIT)

    def local_layer(x_local, logit_local, w_up, w_down):
        n_tok, d_model = x_local.shape
        n_experts = logit_local.shape[1]
        own_experts, _, hid = w_up.shape
        capacity = CAP_FACTOR * n_tok * n_groups // n_experts
        cand = 2 * capacity // n_groups
        half = d_model // 2
        block = lambda n: pltpu.VMEM((n, cand, d_model), jnp.bfloat16)

        small = jax.ShapeDtypeStruct((cand, n_experts), jnp.float32)
        val, idx, gate = pl.pallas_call(
            functools.partial(route_kernel, cand),
            out_shape=(small,) * 3,
            scratch_shapes=[pltpu.VMEM((n_tok, n_experts), jnp.float32), pltpu.VMEM((n_tok, n_experts), jnp.float32)],
        )(logit_local)
        val_send = jnp.pad(val.T, ((0, 0), (0, 128 - cand))).reshape(n_experts, 1, 128)

        z = pl.pallas_call(
            functools.partial(expert_kernel, capacity),
            out_shape=jax.ShapeDtypeStruct((n_groups, cand, d_model), jnp.bfloat16),
            in_specs=[vmem_spec, vmem_spec, any_spec, any_spec, any_spec],
            out_specs=any_spec,
            scratch_shapes=[
                pltpu.VMEM((n_groups * cand, 1), jnp.float32), block(n_groups), block(n_jobs), block(n_jobs), block(n_groups),
                pltpu.VMEM((n_groups, 1, 128), jnp.float32),
                pltpu.VMEM((2, d_model, hid), jnp.bfloat16), pltpu.VMEM((2, hid, d_model), jnp.bfloat16),
                pltpu.VMEM((2, 8, cand, d_model), jnp.bfloat16),
                dma((n_legs,)), dma((n_legs,)), dma((n_jobs,)), dma((n_jobs,)), dma((2,)), dma((2,)), dma((3,)), dma((2,)),
            ],
            compiler_params=params,
        )(idx, x_local, val_send, w_up, w_down)

        return pl.pallas_call(
            combine_kernel,
            out_shape=jax.ShapeDtypeStruct((n_tok, d_model), jnp.bfloat16),
            in_specs=[vmem_spec, vmem_spec, any_spec, any_spec],
            out_specs=any_spec,
            scratch_shapes=[
                pltpu.VMEM((n_groups // 4, 8 * cand), jnp.float32), pltpu.VMEM((n_groups // 4, 8 * cand), jnp.float32),
                block(n_jobs), block(n_jobs),
                pltpu.VMEM((n_groups, own_experts, cand, half), jnp.bfloat16),
                pltpu.VMEM((n_tok, half), jnp.float32), pltpu.VMEM((n_tok, half), jnp.bfloat16), pltpu.VMEM((n_tok, half), jnp.bfloat16),
                dma((n_legs,)), dma((n_legs,)), dma((n_groups,)), dma((n_groups,)), dma((n_groups,)), dma((n_groups,)),
                dma((2,)), dma((4,)), dma((4,)), dma((4,)),
            ],
            compiler_params=params,
        )(idx, gate, x_local, z)

    token_spec = P(("dp", "ep"), None)
    return jax.shard_map(local_layer, mesh=mesh, in_specs=(token_spec, token_spec, P("ep", None, "tp"), P("ep", "tp", None)), out_specs=token_spec, check_vma=False)
```

time: 1020 us -> 312 us (0.31)
  the two profiles are of different devices: /device:TPU:2 before, /device:TPU:1 now
where the time goes in v2:
time: 312 us
  Pallas kernels  306 us (98%)
  local copies, waits for them, and re-layouts  6.24 us (2%)
    pallas_call x1, Pallas kernels, local_layer(): pl.pallas_call(functools.partial(expert_kernel, capacity), out_shape=jax....  154 us
    pallas_call x1, Pallas kernels, local_layer(): pl.pallas_call(combine_kernel, out_shape=jax.ShapeDtypeStruct((n_tok, d_m...  145 us
    pallas_call x1, Pallas kernels, local_layer(): pl.pallas_call(functools.partial(route_kernel, cand), out_shape=(small,)...  7.15 us

profile of v2, /device:TPU:1, one launch (start us, length us, event | category | flops | bytes accessed | tf_op | source)
XLA Modules:
  0.0 311.8 jit_solution(13382730698384721617)
XLA Ops:
  0.0 7.1 %shard_map.46 = (f32[32,128]{1,0:T(8,128)}, f32[32,128]{1,0:T(8,128)}, f32[32,128]{1,0:T(8,128)}) custom-call(f32[1024,128]{1,0:T(8,128)} %logit_ref.1), custom_call_target="tpu_custom_call" | custom-call | tf_op jit(solution)/shard_map/pallas_call | solution.py:417
  7.1 0.8 copy.5
  8.0 0.6 pad.4
  8.6 153.8 %shard_map.47.z_ref = bf16[64,32,2048]{2,1,0:T(8,128)(2,1)} custom-call(f32[32,128]{1,0:T(8,128)} %get-tuple-element.8.idx_ref, bf16[1024,2048]{1,0:T(8,128)(2,1)} %x_ref.3, f32[128,1,128]{2,1,0:T(1,128)} %bitcast.2, bf16[2,2048,384]{2,1,0:T(8,128)(2,1)} %wu_ref.1, bf16[2,384,2048]{2,1,0:T(8,128)(2,1)} %wd_ref.1), custom_call_target="tpu_custom_call" | custom-call | tf_op jit(solution)/shard_map/pallas_call | solution.py:424
  162.4 144.6 %shard_map.48 = bf16[1024,2048]{1,0:T(8,128)(2,1)} custom-call(f32[32,128]{1,0:T(8,128)} %get-tuple-element.8.idx_ref, f32[32,128]{1,0:T(8,128)} %get-tuple-element.9.gate_ref, bf16[1024,2048]{1,0:T(8,128)(2,1)} %x_ref.3, bf16[64,32,2048]{2,1,0:T(8,128)(2,1)} %shard_map.47.z_ref), custom_call_target="tpu_custom_call" | custom-call | tf_op jit(solution)/shard_map/pallas_call | solution.py:439
  307.1 4.8 %copy.7 = bf16[1024,2048]{1,0:T(8,128)(2,1)} copy(bf16[1024,2048]{1,0:T(8,128)(2,1)} %shard_map.48) | data formatting | bytes 8388608

commit v3 on v0

v3 whole, which is shorter than its diff:
```python
import functools

import jax
import jax.numpy as jnp
from jax import lax
from jax.experimental import pallas as pl
from jax.experimental.pallas import tpu as pltpu
from jax.sharding import PartitionSpec as P

CAP_FACTOR = 2
MESH = pl.DeviceIdType.MESH
SIDE = 4
LAG = 12.0
EARLY = 10.0
EARLY_HOP = 6.0
AHEAD = 2.0
DONE_LAG = 5.0
EXPERT_COST = 3.0
PICK_PER, EXPERT_PER, COMBINE_PER = 8, 8, 4
VMEM_LIMIT = 67043328
SELF = (0, 0, 0)


def neg(off):
    return tuple((-v) % SIDE for v in off)


def plan(priority, lag, release, begin):
    jobs = [(p // 16, p // 4 % 4, p % 4) for p in priority]
    dur = {1: 1.0, 3: 1.0, 2: 2.0}
    rem = {o: {d for d in range(3) if o[d]} for o in jobs}
    ready = dict(release)
    count = {o: 0 for o in jobs}
    free = list(begin)
    legs = []
    while any(rem.values()):
        d = min((d for d in range(3) if any(d in rem[o] for o in jobs)), key=lambda d: free[d])
        cand = [o for o in jobs if d in rem[o]]
        avail = [o for o in cand if ready[o] <= free[d] + 1e-9]
        if not avail:
            free[d] = min(ready[o] for o in cand)
            continue
        o = avail[0]
        rem[o].discard(d)
        legs.append((free[d], o, d, count[o]))
        count[o] += 1
        free[d] += dur[o[d]]
        ready[o] = free[d] + lag
    return sorted(legs), {o: ready[o] - lag for o in jobs}, free


OUT_PRIORITY = (3, 39, 31, 61, 40, 26, 34, 58, 44, 51, 33, 12, 27, 62, 41, 4, 22, 17, 21, 11, 52, 23, 45, 60, 7, 49, 18, 36, 35, 13, 57, 32, 43, 15, 47, 59, 8, 55, 5, 46, 10, 24, 54, 50, 20, 9, 38, 29, 2, 63, 28, 1, 14, 56, 53, 42, 48, 37, 6, 30, 25, 19, 16)
BACK_PRIORITY = (7, 37, 39, 47, 6, 58, 28, 13, 23, 24, 57, 11, 4, 22, 1, 43, 27, 32, 41, 2, 63, 52, 62, 59, 61, 60, 17, 3, 38, 36, 26, 16, 19, 34, 42, 49, 21, 53, 29, 14, 31, 46, 30, 54, 20, 35, 33, 12, 45, 51, 10, 25, 8, 9, 48, 56, 15, 18, 50, 5, 40, 44, 55)
OFFSETS = [(a, b, c) for a in range(SIDE) for b in range(SIDE) for c in range(SIDE) if a or b or c]
N_LEGS = {o: sum(1 for v in o if v) for o in OFFSETS}
JOB_ID = {o: j for j, o in enumerate(sorted(OFFSETS, key=lambda o: (-N_LEGS[o], o)))}
N_HOP = [sum(1 for o in OFFSETS if N_LEGS[o] > i) for i in (1, 2)]

OUT_LEGS, OUT_DONE, AXIS_FREE = plan(OUT_PRIORITY, LAG, {o: 0.0 for o in OFFSETS}, (0.0, 0.0, 0.0))
START = {o: t for t, o, _, i in OUT_LEGS if i == 0}
SEND_ORDER = sorted(OFFSETS, key=lambda o: (START[o], o)) + [SELF]
DONE_ORDER = [SELF] + sorted(OFFSETS, key=lambda o: (OUT_DONE[o], o))
SEND_SLOT = {o: p for p, o in enumerate(SEND_ORDER)}
DONE_SLOT = {o: r for r, o in enumerate(DONE_ORDER)}
LEG_ID = {(o, i): k for k, (_, o, _, i) in enumerate(OUT_LEGS)}
N_CHUNK = len(DONE_ORDER) // EXPERT_PER
N_BACK = len(DONE_ORDER) // COMBINE_PER


def chunks(order, per):
    return [order[g:g + per] for g in range(0, len(order), per)]


PICK_TIMES = [min(START[o] for o in c if o != SELF) - EARLY - AHEAD for c in chunks(SEND_ORDER, PICK_PER)]
EXPERT_TIMES = []
for group in chunks(DONE_ORDER, EXPERT_PER):
    at = max(OUT_DONE.get(o, 0.0) for o in group) + DONE_LAG
    EXPERT_TIMES.append(max(at, EXPERT_TIMES[-1] + EXPERT_COST) if EXPERT_TIMES else at)
PICK_TIMES = [min(t, EXPERT_TIMES[0] - 1.0 - 0.01 * (N_CHUNK - g)) for g, t in enumerate(PICK_TIMES)]
RELEASE = {o: EXPERT_TIMES[DONE_SLOT[neg(o)] // EXPERT_PER] + EXPERT_COST + EARLY for o in OFFSETS}
BACK_LEGS, BACK_DONE, _ = plan(BACK_PRIORITY, LAG, RELEASE, AXIS_FREE)
BACK_ID = {(o, i): k for k, (_, o, _, i) in enumerate(BACK_LEGS)}
BACK_ORDER = [SELF] + sorted(OFFSETS, key=lambda o: (BACK_DONE[o], o))
BACK_SLOT = {o: r for r, o in enumerate(BACK_ORDER)}
BACK_TIMES = [max(BACK_DONE.get(o, 0.0) for o in c) + DONE_LAG for c in chunks(BACK_ORDER, COMBINE_PER)]
BACK_TIMES = [max(t, EXPERT_TIMES[-1] + EXPERT_COST) for t in BACK_TIMES]


def group_events():
    rest = [(t - (EARLY_HOP if i else EARLY), kind, (o, axis, i)) for kind, legs in ((0, OUT_LEGS), (1, BACK_LEGS)) for t, o, axis, i in legs]
    rest.sort()
    groups = []
    for t in PICK_TIMES + EXPERT_TIMES + BACK_TIMES:
        groups.append([e[1:] for e in rest if e[0] < t])
        rest = [e for e in rest if e[0] >= t]
    return groups + [[e[1:] for e in rest]]


GROUPS = group_events()


def axis_peers(me, sign):
    z = lax.div(me, SIDE * SIDE)
    y = lax.rem(lax.div(me, SIDE), SIDE)
    x = lax.rem(me, SIDE)
    return [[lax.rem(p + v + sign * (2 * SIDE - 2 * v), SIDE) * scale for v in range(SIDE)] for p, scale in ((z, SIDE * SIDE), (y, SIDE), (x, 1))]


def peer_at(table, off):
    return table[0][off[0]] + table[1][off[1]] + table[2][off[2]]


def leg_peer(table, off, axis):
    return peer_at(table, tuple(v if q == axis else 0 for q, v in enumerate(off)))


def lane_column(table, lane):
    lanes = lax.broadcasted_iota(jnp.int32, table.shape, 1)
    return jnp.sum(jnp.where(lanes == lane, table, 0.0), axis=1, keepdims=True)


def route_kernel(n_cand, logit_ref, val_ref, idx_ref, gate_ref, work, soft):
    n_tok, lanes = logit_ref.shape
    step = 64
    best = jnp.full((8, lanes), -jnp.inf, jnp.float32)
    for lo in range(0, n_tok, step):
        v = logit_ref[lo:lo + step, :]
        e = jnp.exp(v - jnp.max(v, axis=1, keepdims=True))
        soft[lo:lo + step, :] = e / jnp.sum(e, axis=1, keepdims=True)
        work[lo:lo + step, :] = v
        best = jnp.maximum(best, jnp.max(v.reshape(step // 8, 8, lanes), axis=0))
    row = lax.broadcasted_iota(jnp.int32, (step, lanes), 0).astype(jnp.float32)

    def body(k, best):
        top = jnp.max(best, axis=0, keepdims=True)
        nxt = jnp.full((8, lanes), -jnp.inf, jnp.float32)
        pos = jnp.zeros((8, lanes), jnp.float32)
        gat = jnp.zeros((8, lanes), jnp.float32)
        for lo in range(0, n_tok, step):
            v = work[lo:lo + step, :]
            hit = v == top
            v = jnp.where(hit, -jnp.inf, v)
            work[lo:lo + step, :] = v
            nxt = jnp.maximum(nxt, jnp.max(v.reshape(step // 8, 8, lanes), axis=0))
            pos = pos + jnp.sum(jnp.where(hit, row + float(lo), 0.0).reshape(step // 8, 8, lanes), axis=0)
            gat = gat + jnp.sum(jnp.where(hit, soft[lo:lo + step, :], 0.0).reshape(step // 8, 8, lanes), axis=0)
        val_ref[pl.ds(k, 1), :] = top
        idx_ref[pl.ds(k, 1), :] = jnp.sum(pos, axis=0, keepdims=True)
        gate_ref[pl.ds(k, 1), :] = jnp.sum(gat, axis=0, keepdims=True)
        return nxt

    lax.fori_loop(0, n_cand, body, best)


def layer_kernel(capacity, idx_ref, gate_ref, x_ref, val_ref, wu_ref, wd_ref, out_ref, back1, back2,
                 cols, ids, gts, outbox, hop1, hop2, inbox, rval, wu, wd, back, acc, obuf,
                 send, recv, vsend, vrecv, wsend, wrecv, lsem, rsend, rrecv, asend, arecv, bsend, brecv, osend, orecv, osem):
    me, core = lax.axis_index("ep"), lax.axis_index("tp")
    other = 1 - core
    table = axis_peers(me, core)
    tables = [axis_peers(me, p) for p in range(back.shape[1])]
    n_slot, cand, d_model = outbox.shape
    n_par, half = back.shape[1], back.shape[3]
    n_tok, lanes = x_ref.shape[0], val_ref.shape[2]
    own_experts = wu_ref.shape[0]
    rows = EXPERT_PER * cand
    mine = pl.ds(pl.multiple_of(core * half, half), half)
    theirs = pl.ds(pl.multiple_of(other * half, half), half)
    hops, back_hops = (hop1, hop2), (back1, back2)

    weights = []
    for i, (src, dst) in enumerate(((wu_ref, wu), (wd_ref, wd))):
        weights.append(pltpu.make_async_copy(src.at[core], dst.at[0], lsem.at[i]))
        weights.append(pltpu.make_async_remote_copy(src.at[other], dst.at[1], wsend.at[i], wrecv.at[i], device_id={"tp": other}, device_id_type=MESH))
    own_val = pltpu.make_async_copy(val_ref.at[own_experts * me + core], rval.at[DONE_SLOT[SELF]], lsem.at[2])

    def val_copy(o):
        to = peer_at(table, o)
        j = JOB_ID[o]
        return pltpu.make_async_remote_copy(val_ref.at[own_experts * to + core], rval.at[DONE_SLOT[o]], vsend.at[j], vrecv.at[j], device_id={"ep": to}, device_id_type=MESH)

    def whole(s, r):
        return pltpu.make_async_remote_copy(inbox.at[0], inbox.at[0], s, r, device_id={"tp": other}, device_id_type=MESH)

    def part(s, r):
        return pltpu.make_async_remote_copy(back.at[0, 0], back.at[0, 0], s, r, device_id={"tp": other}, device_id_type=MESH)

    def out_leg(o, axis, i):
        if i:
            whole(send.at[0], recv.at[LEG_ID[o, i - 1]]).wait_recv()
        src = hops[i - 1].at[JOB_ID[o]] if i else outbox.at[SEND_SLOT[o]]
        dst = inbox.at[DONE_SLOT[o]] if i == N_LEGS[o] - 1 else hops[i].at[JOB_ID[o]]
        k = LEG_ID[o, i]
        pltpu.make_async_remote_copy(src, dst, send.at[k], recv.at[k], device_id={"ep": leg_peer(table, o, axis)}, device_id_type=MESH).start()

    def split_copy(o, src, h, to):
        cols_of, (s, r) = ((mine, (asend, arecv)), (theirs, (bsend, brecv)))[h]
        j = BACK_SLOT[o]
        there = {} if to is None else {"ep": to}
        if h:
            there["tp"] = other
        return pltpu.make_async_remote_copy(src.at[:, cols_of], back.at[j, core], s.at[j], r.at[j], device_id=there, device_id_type=MESH)

    def back_leg(o, axis, i):
        if i:
            whole(rsend.at[0], rrecv.at[BACK_ID[o, i - 1]]).wait_recv()
        src = back_hops[i - 1].at[JOB_ID[o]] if i else inbox.at[DONE_SLOT[neg(o)]]
        to = leg_peer(table, o, axis)
        if i == N_LEGS[o] - 1:
            for h in range(2):
                split_copy(o, src, h, to).start()
        else:
            k = BACK_ID[o, i]
            pltpu.make_async_remote_copy(src, back_hops[i].at[JOB_ID[o]], rsend.at[k], rrecv.at[k], device_id={"ep": to}, device_id_type=MESH).start()

    def run_legs(group):
        for kind, leg in group:
            (back_leg if kind else out_leg)(*leg)

    idx = idx_ref[...]

    def set_columns(p):
        cols[p * cand:(p + 1) * cand, :] = lane_column(idx, own_experts * peer_at(table, SEND_ORDER[p]) + core)

    def set_rows(g):
        at = []
        for o in BACK_ORDER[g * COMBINE_PER:(g + 1) * COMBINE_PER]:
            for p in range(n_par):
                at.append(own_experts * peer_at(tables[p], neg(o)) + p)
        n = len(at) * cand
        eye = lax.broadcasted_iota(jnp.int32, (n, n), 0) == lax.broadcasted_iota(jnp.int32, (n, n), 1)
        for source, dst in ((idx, ids), (gate_ref[...], gts)):
            col = jnp.concatenate([lane_column(source, e) for e in at], axis=0)
            dst[g:g + 1, :] = jnp.sum(jnp.where(eye, col, 0.0), axis=0, keepdims=True)

    for p in range(PICK_PER):
        set_columns(p)

    def pick(g, c):
        for k in range(N_CHUNK):
            @pl.when(g == k)
            def _():
                run_legs(GROUPS[k])
        at = pl.multiple_of(g * rows, rows)
        onehot = (lax.broadcasted_iota(jnp.int32, (rows, n_tok), 1).astype(jnp.float32) == cols[pl.ds(at, rows), :]).astype(jnp.bfloat16)
        got = jnp.dot(onehot, x_ref[...], preferred_element_type=jnp.float32).astype(jnp.bfloat16)
        outbox[pl.ds(g * PICK_PER, PICK_PER)] = got.reshape(PICK_PER, cand, d_model)
        for k in range(N_CHUNK):
            @pl.when(g == k)
            def _():
                if k == 0:
                    for w in weights + [own_val]:
                        w.start()
                    for o in OFFSETS:
                        val_copy(o).start()
                if k < N_CHUNK - 1:
                    for p in range((k + 1) * PICK_PER, (k + 2) * PICK_PER):
                        set_columns(p)
                for b in range(k * N_BACK // N_CHUNK, (k + 1) * N_BACK // N_CHUNK):
                    set_rows(b)
        return c

    lax.fori_loop(0, N_CHUNK, pick, 0)
    inbox[DONE_SLOT[SELF]] = outbox[SEND_SLOT[SELF]]

    def expert(g, c):
        for k in range(N_CHUNK):
            @pl.when(g == k)
            def _():
                run_legs(GROUPS[N_CHUNK + k])
                if k == 0:
                    for o in OFFSETS:
                        val_copy(o).wait_recv()
                    for w in weights + [own_val]:
                        w.wait()
                for o in DONE_ORDER[k * EXPERT_PER:(k + 1) * EXPERT_PER]:
                    if o != SELF:
                        whole(send.at[0], recv.at[LEG_ID[o, N_LEGS[o] - 1]]).wait_recv()
        eye = lax.broadcasted_iota(jnp.int32, (cand, lanes), 0) == lax.broadcasted_iota(jnp.int32, (cand, lanes), 1)
        value = jnp.concatenate([jnp.sum(jnp.where(eye, rval[g * EXPERT_PER + i], 0.0), axis=1, keepdims=True) for i in range(EXPERT_PER)], axis=0)
        real = lax.broadcasted_iota(jnp.int32, (1, lanes), 1) < cand

        def count(j, total):
            return total + (jnp.where(real, rval[j], -jnp.inf) > value).astype(jnp.float32)

        above = lax.fori_loop(0, n_slot, count, jnp.zeros((rows, lanes), jnp.float32), unroll=8)
        keep = jnp.sum(above, axis=1, keepdims=True) < float(capacity)
        here = pl.ds(g * EXPERT_PER, EXPERT_PER)
        x = inbox[here].reshape(rows, d_model)
        z = None
        for h in range(2):
            pre = jnp.dot(x, wu[h], preferred_element_type=jnp.float32)
            hid = jax.nn.gelu(pre, approximate=True).astype(jnp.bfloat16)
            term = jnp.dot(hid, wd[h], preferred_element_type=jnp.float32)
            z = term if z is None else z + term
        inbox[here] = jnp.where(keep, z, 0.0).astype(jnp.bfloat16).reshape(EXPERT_PER, cand, d_model)
        return c

    lax.fori_loop(0, N_CHUNK, expert, 0)

    def combine(g, c):
        for k in range(N_BACK):
            @pl.when(g == k)
            def _():
                run_legs(GROUPS[2 * N_CHUNK + k])
                if k == 0:
                    for p in range(n_par):
                        @pl.when(core == p)
                        def _():
                            back[BACK_SLOT[SELF], p] = inbox[DONE_SLOT[SELF], :, p * half:(p + 1) * half]
                    split_copy(SELF, inbox.at[DONE_SLOT[SELF]], 1, None).start()
                if k == N_BACK - 1:
                    run_legs(GROUPS[2 * N_CHUNK + N_BACK])
                for o in BACK_ORDER[k * COMBINE_PER:(k + 1) * COMBINE_PER]:
                    j = BACK_SLOT[o]
                    if o != SELF:
                        part(asend.at[j], arecv.at[j]).wait_recv()
                    part(bsend.at[j], brecv.at[j]).wait_recv()
        n = ids.shape[1]
        z = back[pl.ds(g * COMBINE_PER, COMBINE_PER)].reshape(n, half)
        hit = lax.broadcasted_iota(jnp.int32, (n_tok, n), 0).astype(jnp.float32) == ids[pl.ds(g, 1), :]
        left = gts[pl.ds(g, 1), :]
        total = None
        for _ in range(3):
            piece = left.astype(jnp.bfloat16)
            left = left - piece.astype(jnp.float32)
            mat = jnp.where(hit, piece.astype(jnp.float32), 0.0).astype(jnp.bfloat16)
            term = jnp.dot(mat, z, preferred_element_type=jnp.float32)
            total = term if total is None else total + term

        @pl.when(g == 0)
        def _():
            acc[...] = total

        @pl.when(g > 0)
        def _():
            acc[...] += total
        return c

    lax.fori_loop(0, N_BACK, combine, 0)
    n_part = osend.shape[0]
    size = n_tok // n_part

    def out_copies(b):
        at = pl.ds(pl.multiple_of(b * size, size), size)
        src, dst = obuf.at[at], out_ref.at[at, mine]
        return (pltpu.make_async_copy(src, dst, osem.at[b]),
                pltpu.make_async_remote_copy(src, dst, osend.at[b], orecv.at[b], device_id={"tp": other}, device_id_type=MESH))

    def finish(b, c):
        at = pl.ds(pl.multiple_of(b * size, size), size)
        for p in range(n_par):
            @pl.when(core == p)
            def _():
                obuf[at, :] = (x_ref[at, p * half:(p + 1) * half].astype(jnp.float32) + acc[at, :]).astype(jnp.bfloat16)
        for copy in out_copies(b):
            copy.start()
        return c

    lax.fori_loop(0, n_part, finish, 0)

    def drain_legs(k, c):
        whole(send.at[k], recv.at[0]).wait_send()
        return c

    lax.fori_loop(0, len(OUT_LEGS), drain_legs, 0)

    def drain_vals(j, c):
        pltpu.make_async_remote_copy(rval.at[0], rval.at[0], vsend.at[j], vrecv.at[0], device_id={"tp": other}, device_id_type=MESH).wait_send()
        return c

    lax.fori_loop(0, len(OFFSETS), drain_vals, 0)
    for _, o, _, i in BACK_LEGS:
        if i < N_LEGS[o] - 1:
            whole(rsend.at[BACK_ID[o, i]], rrecv.at[0]).wait_send()

    def drain_back(j, c):
        @pl.when(j != BACK_SLOT[SELF])
        def _():
            part(asend.at[j], arecv.at[j]).wait_send()
        part(bsend.at[j], brecv.at[j]).wait_send()
        return c

    lax.fori_loop(0, n_slot, drain_back, 0)

    def drain_out(b, c):
        for copy in out_copies(b):
            copy.wait()
        return c

    lax.fori_loop(0, n_part, drain_out, 0)


def solution(mesh):
    n_groups = mesh.shape["ep"]
    any_spec = pl.BlockSpec(memory_space=pl.ANY)
    vmem_spec = pl.BlockSpec(memory_space=pltpu.VMEM)
    dma = pltpu.SemaphoreType.DMA
    n_legs, n_jobs = len(OUT_LEGS), len(OFFSETS)

    def local_layer(x_local, logit_local, w_up, w_down):
        n_tok, d_model = x_local.shape
        n_experts = logit_local.shape[1]
        own_experts, _, hid = w_up.shape
        capacity = CAP_FACTOR * n_tok * n_groups // n_experts
        cand = 2 * capacity // n_groups
        half = d_model // 2
        n_back_rows = COMBINE_PER * own_experts * cand
        block = lambda n: pltpu.VMEM((n, cand, d_model), jnp.bfloat16)

        small = jax.ShapeDtypeStruct((cand, n_experts), jnp.float32)
        val, idx, gate = pl.pallas_call(
            functools.partial(route_kernel, cand),
            out_shape=(small,) * 3,
            scratch_shapes=[pltpu.VMEM((n_tok, n_experts), jnp.float32), pltpu.VMEM((n_tok, n_experts), jnp.float32)],
        )(logit_local)
        val_send = jnp.pad(val.T, ((0, 0), (0, 128 - cand))).reshape(n_experts, 1, 128)

        out, _, _ = pl.pallas_call(
            functools.partial(layer_kernel, capacity),
            out_shape=(
                jax.ShapeDtypeStruct((n_tok, d_model), jnp.bfloat16),
                jax.ShapeDtypeStruct((N_HOP[0], cand, d_model), jnp.bfloat16),
                jax.ShapeDtypeStruct((N_HOP[1], cand, d_model), jnp.bfloat16),
            ),
            in_specs=[vmem_spec, vmem_spec, vmem_spec, any_spec, any_spec, any_spec],
            out_specs=(any_spec,) * 3,
            scratch_shapes=[
                pltpu.VMEM((n_groups * cand, 1), jnp.float32),
                pltpu.VMEM((N_BACK, n_back_rows), jnp.float32), pltpu.VMEM((N_BACK, n_back_rows), jnp.float32),
                block(n_groups), block(N_HOP[0]), block(N_HOP[1]), block(n_groups),
                pltpu.VMEM((n_groups, 1, 128), jnp.float32),
                pltpu.VMEM((2, d_model, hid), jnp.bfloat16), pltpu.VMEM((2, hid, d_model), jnp.bfloat16),
                pltpu.VMEM((n_groups, own_experts, cand, half), jnp.bfloat16),
                pltpu.VMEM((n_tok, half), jnp.float32), pltpu.VMEM((n_tok, half), jnp.bfloat16),
                dma((n_legs,)), dma((n_legs,)), dma((n_jobs,)), dma((n_jobs,)), dma((2,)), dma((2,)), dma((3,)),
                dma((n_legs,)), dma((n_legs,)), dma((n_groups,)), dma((n_groups,)), dma((n_groups,)), dma((n_groups,)),
                dma((4,)), dma((4,)), dma((4,)),
            ],
            compiler_params=pltpu.CompilerParams(has_side_effects=True, vmem_limit_bytes=VMEM_LIMIT),
        )(idx, gate, x_local, val_send, w_up, w_down)
        return out

    token_spec = P(("dp", "ep"), None)
    return jax.shard_map(local_layer, mesh=mesh, in_specs=(token_spec, token_spec, P("ep", None, "tp"), P("ep", "tp", None)), out_specs=token_spec, check_vma=False)
```

time: 1020 us -> 247 us (0.24)
  the two profiles are of different devices: /device:TPU:2 before, /device:TPU:1 now
where the time goes in v3:
time: 247 us
  Pallas kernels  241 us (98%)
  local copies, waits for them, and re-layouts  6.24 us (3%)
    pallas_call x1, Pallas kernels, local_layer(): pl.pallas_call(functools.partial(layer_kernel, capacity), out_shape=(jax....  234 us
    pallas_call x1, Pallas kernels, local_layer(): pl.pallas_call(functools.partial(route_kernel, cand), out_shape=(small,)...  7.14 us

profile of v3, /device:TPU:1, one launch (start us, length us, event | category | flops | bytes accessed | tf_op | source)
XLA Modules:
  0.0 246.9 jit_solution(9975715220038913174)
XLA Ops:
  0.0 7.1 %shard_map.46 = (f32[32,128]{1,0:T(8,128)}, f32[32,128]{1,0:T(8,128)}, f32[32,128]{1,0:T(8,128)}) custom-call(f32[1024,128]{1,0:T(8,128)} %logit_ref.1), custom_call_target="tpu_custom_call" | custom-call | tf_op jit(solution)/shard_map/pallas_call | solution.py:412
  7.1 0.8 copy.5
  8.0 0.6 pad.4
  8.6 233.5 %shard_map.47 = (bf16[1024,2048]{1,0:T(8,128)(2,1)}, bf16[54,32,2048]{2,1,0:T(8,128)(2,1)}, bf16[27,32,2048]{2,1,0:T(8,128)(2,1)}) custom-call(f32[32,128]{1,0:T(8,128)} %get-tuple-element.9.idx_ref, f32[32,128]{1,0:T(8,128)} %get-tuple-element.10.gate_ref, bf16[1024,2048]{1,0:T(8,128)(2,1)} %x_ref.1, f32[128,1,128]{2,1,0:T(1,128)} %bitcast.2, ...), custom_call_target="tpu_custom_call" | custom-call | tf_op jit(solution)/shard_map/pallas_call | solution.py:419
  242.1 4.8 %copy.7 = bf16[1024,2048]{1,0:T(8,128)(2,1)} copy(bf16[1024,2048]{1,0:T(8,128)(2,1)} %get-tuple-element.12) | data formatting | bytes 8388608

commit v4 on v3

--- a/solution.py
+++ b/solution.py
@@ -119,7 +119,7 @@
     return jnp.sum(jnp.where(lanes == lane, table, 0.0), axis=1, keepdims=True)
 
 
-def route_kernel(n_cand, logit_ref, val_ref, idx_ref, gate_ref, work, soft):
+def route(n_cand, logit_ref, val_ref, idx_ref, gate_ref, work, soft):
     n_tok, lanes = logit_ref.shape
     step = 64
     best = jnp.full((8, lanes), -jnp.inf, jnp.float32)
@@ -152,32 +152,39 @@
     lax.fori_loop(0, n_cand, body, best)
 
 
-def layer_kernel(capacity, idx_ref, gate_ref, x_ref, val_ref, wu_ref, wd_ref, out_ref, back1, back2,
-                 cols, ids, gts, outbox, hop1, hop2, inbox, rval, wu, wd, back, acc, obuf,
-                 send, recv, vsend, vrecv, wsend, wrecv, lsem, rsend, rrecv, asend, arecv, bsend, brecv, osend, orecv, osem):
+def layer_kernel(capacity, logit_ref, x_hbm, wu_ref, wd_ref, out_ref, back1, back2,
+                 x_ref, val_tab, idx_tab, gate_tab, work, soft, vals, cols, ids, gts, outbox, hop1, hop2, inbox, rval, wu, wd, back, acc, obuf,
+                 send, recv, vsend, vrecv, wsend, wrecv, lsem, rsend, rrecv, asend, arecv, bsend, brecv, osend, orecv, osem, xsem):
     me, core = lax.axis_index("ep"), lax.axis_index("tp")
     other = 1 - core
     table = axis_peers(me, core)
     tables = [axis_peers(me, p) for p in range(back.shape[1])]
     n_slot, cand, d_model = outbox.shape
     n_par, half = back.shape[1], back.shape[3]
-    n_tok, lanes = x_ref.shape[0], val_ref.shape[2]
+    n_tok, lanes = x_ref.shape[0], vals.shape[2]
     own_experts = wu_ref.shape[0]
     rows = EXPERT_PER * cand
     mine = pl.ds(pl.multiple_of(core * half, half), half)
     theirs = pl.ds(pl.multiple_of(other * half, half), half)
     hops, back_hops = (hop1, hop2), (back1, back2)
 
+    barrier = pltpu.get_barrier_semaphore()
+    greet = [{"ep": peer_at(table, o)} for o in OFFSETS]
+    greet += [{"ep": peer_at(table, o), "tp": other} for o in OFFSETS if N_LEGS[o] == 1] + [{"tp": other}]
+    for there in greet:
+        pl.semaphore_signal(barrier, inc=1, device_id=there, device_id_type=MESH)
+    x_copy = pltpu.make_async_copy(x_hbm, x_ref, xsem)
+    x_copy.start()
+    route(cand, logit_ref, val_tab, idx_tab, gate_tab, work, soft)
+
     weights = []
     for i, (src, dst) in enumerate(((wu_ref, wu), (wd_ref, wd))):
         weights.append(pltpu.make_async_copy(src.at[core], dst.at[0], lsem.at[i]))
         weights.append(pltpu.make_async_remote_copy(src.at[other], dst.at[1], wsend.at[i], wrecv.at[i], device_id={"tp": other}, device_id_type=MESH))
-    own_val = pltpu.make_async_copy(val_ref.at[own_experts * me + core], rval.at[DONE_SLOT[SELF]], lsem.at[2])
-
     def val_copy(o):
         to = peer_at(table, o)
         j = JOB_ID[o]
-        return pltpu.make_async_remote_copy(val_ref.at[own_experts * to + core], rval.at[DONE_SLOT[o]], vsend.at[j], vrecv.at[j], device_id={"ep": to}, device_id_type=MESH)
+        return pltpu.make_async_remote_copy(vals.at[SEND_SLOT[o]], rval.at[DONE_SLOT[o]], vsend.at[j], vrecv.at[j], device_id={"ep": to}, device_id_type=MESH)
 
     def whole(s, r):
         return pltpu.make_async_remote_copy(inbox.at[0], inbox.at[0], s, r, device_id={"tp": other}, device_id_type=MESH)
@@ -217,10 +224,13 @@
         for kind, leg in group:
             (back_leg if kind else out_leg)(*leg)
 
-    idx = idx_ref[...]
+    val, idx, gate = val_tab[...], idx_tab[...], gate_tab[...]
+    diagonal = lax.broadcasted_iota(jnp.int32, (cand, lanes), 0) == lax.broadcasted_iota(jnp.int32, (cand, lanes), 1)
 
     def set_columns(p):
-        cols[p * cand:(p + 1) * cand, :] = lane_column(idx, own_experts * peer_at(table, SEND_ORDER[p]) + core)
+        e = own_experts * peer_at(table, SEND_ORDER[p]) + core
+        cols[p * cand:(p + 1) * cand, :] = lane_column(idx, e)
+        vals[p] = jnp.sum(jnp.where(diagonal, lane_column(val, e), 0.0), axis=0, keepdims=True)
 
     def set_rows(g):
         at = []
@@ -229,39 +239,47 @@
                 at.append(own_experts * peer_at(tables[p], neg(o)) + p)
         n = len(at) * cand
         eye = lax.broadcasted_iota(jnp.int32, (n, n), 0) == lax.broadcasted_iota(jnp.int32, (n, n), 1)
-        for source, dst in ((idx, ids), (gate_ref[...], gts)):
+        for source, dst in ((idx, ids), (gate, gts)):
             col = jnp.concatenate([lane_column(source, e) for e in at], axis=0)
             dst[g:g + 1, :] = jnp.sum(jnp.where(eye, col, 0.0), axis=0, keepdims=True)
 
     for p in range(PICK_PER):
         set_columns(p)
-
-    def pick(g, c):
-        for k in range(N_CHUNK):
-            @pl.when(g == k)
-            def _():
-                run_legs(GROUPS[k])
+    x_copy.wait()
+
+    def gather(g):
         at = pl.multiple_of(g * rows, rows)
         onehot = (lax.broadcasted_iota(jnp.int32, (rows, n_tok), 1).astype(jnp.float32) == cols[pl.ds(at, rows), :]).astype(jnp.bfloat16)
         got = jnp.dot(onehot, x_ref[...], preferred_element_type=jnp.float32).astype(jnp.bfloat16)
         outbox[pl.ds(g * PICK_PER, PICK_PER)] = got.reshape(PICK_PER, cand, d_model)
-        for k in range(N_CHUNK):
+
+    gather(0)
+    pl.semaphore_wait(barrier, len(greet))
+
+    def pick(g, c):
+        for k in range(1, N_CHUNK):
             @pl.when(g == k)
             def _():
-                if k == 0:
-                    for w in weights + [own_val]:
+                run_legs(GROUPS[0] + GROUPS[1] if k == 1 else GROUPS[k])
+                if k == 1:
+                    for w in weights:
                         w.start()
+                    for p in range(PICK_PER, n_slot):
+                        set_columns(p)
+        gather(g)
+        for k in range(1, N_CHUNK):
+            @pl.when(g == k)
+            def _():
+                if k == 1:
                     for o in OFFSETS:
                         val_copy(o).start()
-                if k < N_CHUNK - 1:
-                    for p in range((k + 1) * PICK_PER, (k + 2) * PICK_PER):
-                        set_columns(p)
-                for b in range(k * N_BACK // N_CHUNK, (k + 1) * N_BACK // N_CHUNK):
+                for b in range((k - 1) * N_BACK // (N_CHUNK - 1), k * N_BACK // (N_CHUNK - 1)):
                     set_rows(b)
         return c
 
-    lax.fori_loop(0, N_CHUNK, pick, 0)
+    lax.fori_loop(1, N_CHUNK, pick, 0)
     inbox[DONE_SLOT[SELF]] = outbox[SEND_SLOT[SELF]]
+    rval[DONE_SLOT[SELF]] = vals[SEND_SLOT[SELF]]
 
     def expert(g, c):
         for k in range(N_CHUNK):
@@ -271,7 +289,7 @@
                 if k == 0:
                     for o in OFFSETS:
                         val_copy(o).wait_recv()
-                    for w in weights + [own_val]:
+                    for w in weights:
                         w.wait()
                 for o in DONE_ORDER[k * EXPERT_PER:(k + 1) * EXPERT_PER]:
                     if o != SELF:
@@ -407,14 +425,8 @@
         half = d_model // 2
         n_back_rows = COMBINE_PER * own_experts * cand
         block = lambda n: pltpu.VMEM((n, cand, d_model), jnp.bfloat16)
-
-        small = jax.ShapeDtypeStruct((cand, n_experts), jnp.float32)
-        val, idx, gate = pl.pallas_call(
-            functools.partial(route_kernel, cand),
-            out_shape=(small,) * 3,
-            scratch_shapes=[pltpu.VMEM((n_tok, n_experts), jnp.float32), pltpu.VMEM((n_tok, n_experts), jnp.float32)],
-        )(logit_local)
-        val_send = jnp.pad(val.T, ((0, 0), (0, 128 - cand))).reshape(n_experts, 1, 128)
+        table = pltpu.VMEM((cand, n_experts), jnp.float32)
+        score = pltpu.VMEM((n_tok, n_experts), jnp.float32)
 
         out, _, _ = pl.pallas_call(
             functools.partial(layer_kernel, capacity),
@@ -423,9 +435,12 @@
                 jax.ShapeDtypeStruct((N_HOP[0], cand, d_model), jnp.bfloat16),
                 jax.ShapeDtypeStruct((N_HOP[1], cand, d_model), jnp.bfloat16),
             ),
-            in_specs=[vmem_spec, vmem_spec, vmem_spec, any_spec, any_spec, any_spec],
+            in_specs=[vmem_spec, any_spec, any_spec, any_spec],
             out_specs=(any_spec,) * 3,
             scratch_shapes=[
+                pltpu.VMEM((n_tok, d_model), jnp.bfloat16),
+                table, table, table, score, score,
+                pltpu.VMEM((n_groups, 1, 128), jnp.float32),
                 pltpu.VMEM((n_groups * cand, 1), jnp.float32),
                 pltpu.VMEM((N_BACK, n_back_rows), jnp.float32), pltpu.VMEM((N_BACK, n_back_rows), jnp.float32),
                 block(n_groups), block(N_HOP[0]), block(N_HOP[1]), block(n_groups),
@@ -433,12 +448,12 @@
                 pltpu.VMEM((2, d_model, hid), jnp.bfloat16), pltpu.VMEM((2, hid, d_model), jnp.bfloat16),
                 pltpu.VMEM((n_groups, own_experts, cand, half), jnp.bfloat16),
                 pltpu.VMEM((n_tok, half), jnp.float32), pltpu.VMEM((n_tok, half), jnp.bfloat16),
-                dma((n_legs,)), dma((n_legs,)), dma((n_jobs,)), dma((n_jobs,)), dma((2,)), dma((2,)), dma((3,)),
+                dma((n_legs,)), dma((n_legs,)), dma((n_jobs,)), dma((n_jobs,)), dma((2,)), dma((2,)), dma((2,)),
                 dma((n_legs,)), dma((n_legs,)), dma((n_groups,)), dma((n_groups,)), dma((n_groups,)), dma((n_groups,)),
-                dma((4,)), dma((4,)), dma((4,)),
+                dma((4,)), dma((4,)), dma((4,)), dma,
             ],
-            compiler_params=pltpu.CompilerParams(has_side_effects=True, vmem_limit_bytes=VMEM_LIMIT),
-        )(idx, gate, x_local, val_send, w_up, w_down)
+            compiler_params=pltpu.CompilerParams(collective_id=0, has_side_effects=True, vmem_limit_bytes=VMEM_LIMIT),
+        )(logit_local, x_local, w_up, w_down)
         return out
 
     token_spec = P(("dp", "ep"), None)

time: 247 us -> 233 us (0.943)
  Pallas kernels: 241 us -> 228 us
    pallas_call x1 -> x0, Pallas kernels: 7.14 us -> none  [local_layer(): pl.pallas_call(functools.partial(route_kernel, cand), out_shape=(small,)...]
    pallas_call x1, Pallas kernels: 234 us -> 228 us  [local_layer(): pl.pallas_call(functools.partial(layer_kernel, capacity), out_shape=(jax....]
where the time goes in v4:
time: 233 us
  Pallas kernels  228 us (98%)
  local copies, waits for them, and re-layouts  4.79 us (2%)
    pallas_call x1, Pallas kernels, local_layer(): pl.pallas_call(functools.partial(layer_kernel, capacity), out_shape=(jax....  228 us
    unnamed x1, local copies, waits for them, and re-layouts  4.79 us

profile of v4, /device:TPU:1, one launch (start us, length us, event | category | flops | bytes accessed | tf_op | source)
XLA Modules:
  0.0 233.0 jit_solution(1199997081892139029)
XLA Ops:
  0.0 228.2 %shard_map.46 = (bf16[1024,2048]{1,0:T(8,128)(2,1)}, bf16[54,32,2048]{2,1,0:T(8,128)(2,1)}, bf16[27,32,2048]{2,1,0:T(8,128)(2,1)}) custom-call(f32[1024,128]{1,0:T(8,128)} %logit_ref.1, bf16[1024,2048]{1,0:T(8,128)(2,1)} %x_hbm.1, bf16[2,2048,384]{2,1,0:T(8,128)(2,1)} %wu_ref.1, bf16[2,384,2048]{2,1,0:T(8,128)(2,1)} %wd_ref.1), custom_call_target="tpu_custom_call" | custom-call | tf_op jit(solution)/shard_map/pallas_call | solution.py:431
  228.2 4.8 %copy.6 = bf16[1024,2048]{1,0:T(8,128)(2,1)} copy(bf16[1024,2048]{1,0:T(8,128)(2,1)} %get-tuple-element.6) | data formatting | bytes 8388608

commit v5 on v4

--- a/solution.py
+++ b/solution.py
@@ -10,12 +10,12 @@
 CAP_FACTOR = 2
 MESH = pl.DeviceIdType.MESH
 SIDE = 4
-LAG = 12.0
-EARLY = 10.0
-EARLY_HOP = 6.0
+LAG = 10.0
+EARLY = 8.0
+EARLY_HOP = 8.0
 AHEAD = 2.0
 DONE_LAG = 5.0
-EXPERT_COST = 3.0
+EXPERT_COST = 3.5
 PICK_PER, EXPERT_PER, COMBINE_PER = 8, 8, 4
 VMEM_LIMIT = 67043328
 SELF = (0, 0, 0)
@@ -49,8 +49,8 @@
     return sorted(legs), {o: ready[o] - lag for o in jobs}, free
 
 
-OUT_PRIORITY = (3, 39, 31, 61, 40, 26, 34, 58, 44, 51, 33, 12, 27, 62, 41, 4, 22, 17, 21, 11, 52, 23, 45, 60, 7, 49, 18, 36, 35, 13, 57, 32, 43, 15, 47, 59, 8, 55, 5, 46, 10, 24, 54, 50, 20, 9, 38, 29, 2, 63, 28, 1, 14, 56, 53, 42, 48, 37, 6, 30, 25, 19, 16)
-BACK_PRIORITY = (7, 37, 39, 47, 6, 58, 28, 13, 23, 24, 57, 11, 4, 22, 1, 43, 27, 32, 41, 2, 63, 52, 62, 59, 61, 60, 17, 3, 38, 36, 26, 16, 19, 34, 42, 49, 21, 53, 29, 14, 31, 46, 30, 54, 20, 35, 33, 12, 45, 51, 10, 25, 8, 9, 48, 56, 15, 18, 50, 5, 40, 44, 55)
+OUT_PRIORITY = (47, 11, 14, 4, 51, 20, 56, 18, 1, 48, 62, 29, 44, 16, 37, 30, 10, 19, 12, 33, 63, 49, 9, 17, 25, 5, 32, 50, 36, 15, 57, 38, 52, 53, 2, 3, 21, 23, 8, 22, 26, 45, 7, 31, 59, 27, 43, 46, 54, 42, 55, 28, 35, 41, 6, 39, 58, 40, 61, 60, 24, 13, 34)
+BACK_PRIORITY = (10, 4, 39, 12, 16, 63, 27, 47, 7, 38, 21, 8, 51, 60, 44, 24, 11, 1, 29, 18, 55, 50, 35, 20, 23, 41, 62, 36, 56, 48, 45, 59, 15, 58, 31, 43, 61, 26, 32, 19, 49, 14, 25, 53, 2, 46, 9, 52, 34, 17, 6, 22, 3, 54, 37, 30, 40, 42, 57, 5, 28, 13, 33)
 OFFSETS = [(a, b, c) for a in range(SIDE) for b in range(SIDE) for c in range(SIDE) if a or b or c]
 N_LEGS = {o: sum(1 for v in o if v) for o in OFFSETS}
 JOB_ID = {o: j for j, o in enumerate(sorted(OFFSETS, key=lambda o: (-N_LEGS[o], o)))}
@@ -119,37 +119,54 @@
     return jnp.sum(jnp.where(lanes == lane, table, 0.0), axis=1, keepdims=True)
 
 
-def route(n_cand, logit_ref, val_ref, idx_ref, gate_ref, work, soft):
+def route(n_cand, logit_ref, val_ref, idx_ref, work):
     n_tok, lanes = logit_ref.shape
     step = 64
+    fold = lambda v: v.reshape(step // 8, 8, lanes)
     best = jnp.full((8, lanes), -jnp.inf, jnp.float32)
     for lo in range(0, n_tok, step):
         v = logit_ref[lo:lo + step, :]
-        e = jnp.exp(v - jnp.max(v, axis=1, keepdims=True))
-        soft[lo:lo + step, :] = e / jnp.sum(e, axis=1, keepdims=True)
         work[lo:lo + step, :] = v
-        best = jnp.maximum(best, jnp.max(v.reshape(step // 8, 8, lanes), axis=0))
+        best = jnp.maximum(best, jnp.max(fold(v), axis=0))
     row = lax.broadcasted_iota(jnp.int32, (step, lanes), 0).astype(jnp.float32)
 
     def body(k, best):
         top = jnp.max(best, axis=0, keepdims=True)
         nxt = jnp.full((8, lanes), -jnp.inf, jnp.float32)
         pos = jnp.zeros((8, lanes), jnp.float32)
-        gat = jnp.zeros((8, lanes), jnp.float32)
         for lo in range(0, n_tok, step):
             v = work[lo:lo + step, :]
             hit = v == top
             v = jnp.where(hit, -jnp.inf, v)
             work[lo:lo + step, :] = v
-            nxt = jnp.maximum(nxt, jnp.max(v.reshape(step // 8, 8, lanes), axis=0))
-            pos = pos + jnp.sum(jnp.where(hit, row + float(lo), 0.0).reshape(step // 8, 8, lanes), axis=0)
-            gat = gat + jnp.sum(jnp.where(hit, soft[lo:lo + step, :], 0.0).reshape(step // 8, 8, lanes), axis=0)
+            nxt = jnp.maximum(nxt, jnp.max(fold(v), axis=0))
+            pos = pos + jnp.sum(fold(jnp.where(hit, row + float(lo), 0.0)), axis=0)
         val_ref[pl.ds(k, 1), :] = top
         idx_ref[pl.ds(k, 1), :] = jnp.sum(pos, axis=0, keepdims=True)
-        gate_ref[pl.ds(k, 1), :] = jnp.sum(gat, axis=0, keepdims=True)
         return nxt
 
     lax.fori_loop(0, n_cand, body, best)
+
+
+def gates(n_cand, logit_ref, idx_ref, gate_ref, soft):
+    n_tok, lanes = logit_ref.shape
+    step = 64
+    for lo in range(0, n_tok, step):
+        v = logit_ref[lo:lo + step, :]
+        e = jnp.exp(v - jnp.max(v, axis=1, keepdims=True))
+        soft[lo:lo + step, :] = e / jnp.sum(e, axis=1, keepdims=True)
+    row = lax.broadcasted_iota(jnp.int32, (step, lanes), 0).astype(jnp.float32)
+
+    def body(k, c):
+        at = idx_ref[pl.ds(k, 1), :]
+        total = jnp.zeros((8, lanes), jnp.float32)
+        for lo in range(0, n_tok, step):
+            mine = jnp.where(row == at - float(lo), soft[lo:lo + step, :], 0.0)
+            total = total + jnp.sum(mine.reshape(step // 8, 8, lanes), axis=0)
+        gate_ref[pl.ds(k, 1), :] = jnp.sum(total, axis=0, keepdims=True)
+        return c
+
+    lax.fori_loop(0, n_cand, body, 0)
 
 
 def layer_kernel(capacity, logit_ref, x_hbm, wu_ref, wd_ref, out_ref, back1, back2,
@@ -175,7 +192,7 @@
         pl.semaphore_signal(barrier, inc=1, device_id=there, device_id_type=MESH)
     x_copy = pltpu.make_async_copy(x_hbm, x_ref, xsem)
     x_copy.start()
-    route(cand, logit_ref, val_tab, idx_tab, gate_tab, work, soft)
+    route(cand, logit_ref, val_tab, idx_tab, work)
 
     weights = []
     for i, (src, dst) in enumerate(((wu_ref, wu), (wd_ref, wd))):
@@ -224,13 +241,16 @@
         for kind, leg in group:
             (back_leg if kind else out_leg)(*leg)
 
-    val, idx, gate = val_tab[...], idx_tab[...], gate_tab[...]
-    diagonal = lax.broadcasted_iota(jnp.int32, (cand, lanes), 0) == lax.broadcasted_iota(jnp.int32, (cand, lanes), 1)
+    val, idx = val_tab[...], idx_tab[...]
+    pack = lanes // cand
+    slot_row = lax.broadcasted_iota(jnp.int32, (cand, lanes), 0)
+    slot_lane = lax.broadcasted_iota(jnp.int32, (cand, lanes), 1)
 
     def set_columns(p):
         e = own_experts * peer_at(table, SEND_ORDER[p]) + core
         cols[p * cand:(p + 1) * cand, :] = lane_column(idx, e)
-        vals[p] = jnp.sum(jnp.where(diagonal, lane_column(val, e), 0.0), axis=0, keepdims=True)
+        at = DONE_SLOT[SEND_ORDER[p]] % pack * cand
+        vals[p] = jnp.sum(jnp.where(slot_lane == slot_row + at, lane_column(val, e), 0.0), axis=0, keepdims=True)
 
     def set_rows(g):
         at = []
@@ -239,7 +259,7 @@
                 at.append(own_experts * peer_at(tables[p], neg(o)) + p)
         n = len(at) * cand
         eye = lax.broadcasted_iota(jnp.int32, (n, n), 0) == lax.broadcasted_iota(jnp.int32, (n, n), 1)
-        for source, dst in ((idx, ids), (gate, gts)):
+        for source, dst in ((idx, ids), (gate_tab[...], gts)):
             col = jnp.concatenate([lane_column(source, e) for e in at], axis=0)
             dst[g:g + 1, :] = jnp.sum(jnp.where(eye, col, 0.0), axis=0, keepdims=True)
 
@@ -253,6 +273,7 @@
         got = jnp.dot(onehot, x_ref[...], preferred_element_type=jnp.float32).astype(jnp.bfloat16)
         outbox[pl.ds(g * PICK_PER, PICK_PER)] = got.reshape(PICK_PER, cand, d_model)
 
+    half_way = N_CHUNK // 2
     gather(0)
     pl.semaphore_wait(barrier, len(greet))
 
@@ -264,17 +285,23 @@
                 if k == 1:
                     for w in weights:
                         w.start()
-                    for p in range(PICK_PER, n_slot):
+                for p in range(k * PICK_PER, (k + 1) * PICK_PER):
+                    if k <= half_way:
                         set_columns(p)
         gather(g)
         for k in range(1, N_CHUNK):
             @pl.when(g == k)
             def _():
-                if k == 1:
+                if k == half_way:
+                    for p in range((k + 1) * PICK_PER, n_slot):
+                        set_columns(p)
                     for o in OFFSETS:
                         val_copy(o).start()
-                for b in range((k - 1) * N_BACK // (N_CHUNK - 1), k * N_BACK // (N_CHUNK - 1)):
-                    set_rows(b)
+                    gates(cand, logit_ref, idx_tab, gate_tab, soft)
+                if k >= half_way:
+                    share = N_BACK // (N_CHUNK - half_way)
+                    for b in range((k - half_way) * share, (k - half_way + 1) * share):
+                        set_rows(b)
         return c
 
     lax.fori_loop(1, N_CHUNK, pick, 0)
@@ -294,14 +321,16 @@
                 for o in DONE_ORDER[k * EXPERT_PER:(k + 1) * EXPERT_PER]:
                     if o != SELF:
                         whole(send.at[0], recv.at[LEG_ID[o, N_LEGS[o] - 1]]).wait_recv()
-        eye = lax.broadcasted_iota(jnp.int32, (cand, lanes), 0) == lax.broadcasted_iota(jnp.int32, (cand, lanes), 1)
-        value = jnp.concatenate([jnp.sum(jnp.where(eye, rval[g * EXPERT_PER + i], 0.0), axis=1, keepdims=True) for i in range(EXPERT_PER)], axis=0)
-        real = lax.broadcasted_iota(jnp.int32, (1, lanes), 1) < cand
+        own = lax.rem(slot_lane, cand) == slot_row
+        value = jnp.concatenate([jnp.sum(jnp.where(own, rval[g * EXPERT_PER + i], 0.0), axis=1, keepdims=True) for i in range(EXPERT_PER)], axis=0)
 
         def count(j, total):
-            return total + (jnp.where(real, rval[j], -jnp.inf) > value).astype(jnp.float32)
-
-        above = lax.fori_loop(0, n_slot, count, jnp.zeros((rows, lanes), jnp.float32), unroll=8)
+            packed = rval[j * pack]
+            for i in range(1, pack):
+                packed = packed + rval[j * pack + i]
+            return total + (packed > value).astype(jnp.float32)
+
+        above = lax.fori_loop(0, n_slot // pack, count, jnp.zeros((rows, lanes), jnp.float32), unroll=4)
         keep = jnp.sum(above, axis=1, keepdims=True) < float(capacity)
         here = pl.ds(g * EXPERT_PER, EXPERT_PER)
         x = inbox[here].reshape(rows, d_model)
@@ -316,27 +345,27 @@
 
     lax.fori_loop(0, N_CHUNK, expert, 0)
 
-    def combine(g, c):
-        for k in range(N_BACK):
-            @pl.when(g == k)
-            def _():
-                run_legs(GROUPS[2 * N_CHUNK + k])
-                if k == 0:
-                    for p in range(n_par):
-                        @pl.when(core == p)
-                        def _():
-                            back[BACK_SLOT[SELF], p] = inbox[DONE_SLOT[SELF], :, p * half:(p + 1) * half]
-                    split_copy(SELF, inbox.at[DONE_SLOT[SELF]], 1, None).start()
-                if k == N_BACK - 1:
-                    run_legs(GROUPS[2 * N_CHUNK + N_BACK])
-                for o in BACK_ORDER[k * COMBINE_PER:(k + 1) * COMBINE_PER]:
-                    j = BACK_SLOT[o]
-                    if o != SELF:
-                        part(asend.at[j], arecv.at[j]).wait_recv()
-                    part(bsend.at[j], brecv.at[j]).wait_recv()
+    def await_rows(k):
+        run_legs(GROUPS[2 * N_CHUNK + k])
+        if k == 0:
+            for p in range(n_par):
+                @pl.when(core == p)
+                def _():
+                    back[BACK_SLOT[SELF], p] = inbox[DONE_SLOT[SELF], :, p * half:(p + 1) * half]
+            split_copy(SELF, inbox.at[DONE_SLOT[SELF]], 1, None).start()
+        if k == N_BACK - 1:
+            run_legs(GROUPS[2 * N_CHUNK + N_BACK])
+        for o in BACK_ORDER[k * COMBINE_PER:(k + 1) * COMBINE_PER]:
+            j = BACK_SLOT[o]
+            if o != SELF:
+                part(asend.at[j], arecv.at[j]).wait_recv()
+            part(bsend.at[j], brecv.at[j]).wait_recv()
+
+    def gated_sum(g, first, count):
         n = ids.shape[1]
         z = back[pl.ds(g * COMBINE_PER, COMBINE_PER)].reshape(n, half)
-        hit = lax.broadcasted_iota(jnp.int32, (n_tok, n), 0).astype(jnp.float32) == ids[pl.ds(g, 1), :]
+        token = lax.broadcasted_iota(jnp.int32, (count, n), 0) + first
+        hit = token.astype(jnp.float32) == ids[pl.ds(g, 1), :]
         left = gts[pl.ds(g, 1), :]
         total = None
         for _ in range(3):
@@ -345,6 +374,14 @@
             mat = jnp.where(hit, piece.astype(jnp.float32), 0.0).astype(jnp.bfloat16)
             term = jnp.dot(mat, z, preferred_element_type=jnp.float32)
             total = term if total is None else total + term
+        return total
+
+    def combine(g, c):
+        for k in range(N_BACK - 1):
+            @pl.when(g == k)
+            def _():
+                await_rows(k)
+        total = gated_sum(g, 0, n_tok)
 
         @pl.when(g == 0)
         def _():
@@ -355,7 +392,8 @@
             acc[...] += total
         return c
 
-    lax.fori_loop(0, N_BACK, combine, 0)
+    lax.fori_loop(0, N_BACK - 1, combine, 0)
+    await_rows(N_BACK - 1)
     n_part = osend.shape[0]
     size = n_tok // n_part
 
@@ -367,10 +405,11 @@
 
     def finish(b, c):
         at = pl.ds(pl.multiple_of(b * size, size), size)
+        y = acc[at, :] + gated_sum(N_BACK - 1, b * size, size)
         for p in range(n_par):
             @pl.when(core == p)
             def _():
-                obuf[at, :] = (x_ref[at, p * half:(p + 1) * half].astype(jnp.float32) + acc[at, :]).astype(jnp.bfloat16)
+                obuf[at, :] = (x_ref[at, p * half:(p + 1) * half].astype(jnp.float32) + y).astype(jnp.bfloat16)
         for copy in out_copies(b):
             copy.start()
         return c

time: 233 us -> 220 us (0.944)
  Pallas kernels: 228 us -> 214 us
    pallas_call x1, Pallas kernels: 228 us -> 214 us  [local_layer(): pl.pallas_call(functools.partial(layer_kernel, capacity), out_shape=(jax....]
where the time goes in v5:
time: 220 us; the launch traced here: 218 us
  Pallas kernels  214 us (97%)
  local copies, waits for them, and re-layouts  4.79 us (2%)
    pallas_call x1, Pallas kernels, local_layer(): pl.pallas_call(functools.partial(layer_kernel, capacity), out_shape=(jax....  214 us
    unnamed x1, local copies, waits for them, and re-layouts  4.79 us

profile of v5, /device:TPU:1, one launch (start us, length us, event | category | flops | bytes accessed | tf_op | source)
XLA Modules:
  0.0 218.3 jit_solution(10000603634602779111)
XLA Ops:
  0.0 213.5 %shard_map.46 = (bf16[1024,2048]{1,0:T(8,128)(2,1)}, bf16[54,32,2048]{2,1,0:T(8,128)(2,1)}, bf16[27,32,2048]{2,1,0:T(8,128)(2,1)}) custom-call(f32[1024,128]{1,0:T(8,128)} %logit_ref.1, bf16[1024,2048]{1,0:T(8,128)(2,1)} %x_hbm.1, bf16[2,2048,384]{2,1,0:T(8,128)(2,1)} %wu_ref.1, bf16[2,384,2048]{2,1,0:T(8,128)(2,1)} %wd_ref.1), custom_call_target="tpu_custom_call" | custom-call | tf_op jit(solution)/shard_map/pallas_call | solution.py:470
  213.5 4.8 %copy.6 = bf16[1024,2048]{1,0:T(8,128)(2,1)} copy(bf16[1024,2048]{1,0:T(8,128)(2,1)} %get-tuple-element.6) | data formatting | bytes 8388608

commit v6 on v5

--- a/solution.py
+++ b/solution.py
@@ -17,7 +17,7 @@
 DONE_LAG = 5.0
 EXPERT_COST = 3.5
 PICK_PER, EXPERT_PER, COMBINE_PER = 8, 8, 4
-VMEM_LIMIT = 67043328
+VMEM_LIMIT = 59 * 1024 * 1024
 SELF = (0, 0, 0)
 
 
@@ -170,8 +170,8 @@
 
 
 def layer_kernel(capacity, logit_ref, x_hbm, wu_ref, wd_ref, out_ref, back1, back2,
-                 x_ref, val_tab, idx_tab, gate_tab, work, soft, vals, cols, ids, gts, outbox, hop1, hop2, inbox, rval, wu, wd, back, acc, obuf,
-                 send, recv, vsend, vrecv, wsend, wrecv, lsem, rsend, rrecv, asend, arecv, bsend, brecv, osend, orecv, osem, xsem):
+                 x_ref, val_tab, idx_tab, gate_tab, work, soft, vals, cols, ids, gts, outbox, hop1, hop2, inbox, rval, wu, wd, back, acc,
+                 send, recv, vsend, vrecv, wsend, wrecv, lsem, rsend, rrecv, asend, arecv, bsend, brecv, osend, orecv, xsem):
     me, core = lax.axis_index("ep"), lax.axis_index("tp")
     other = 1 - core
     table = axis_peers(me, core)
@@ -399,9 +399,8 @@
 
     def out_copies(b):
         at = pl.ds(pl.multiple_of(b * size, size), size)
-        src, dst = obuf.at[at], out_ref.at[at, mine]
-        return (pltpu.make_async_copy(src, dst, osem.at[b]),
-                pltpu.make_async_remote_copy(src, dst, osend.at[b], orecv.at[b], device_id={"tp": other}, device_id_type=MESH))
+        half_of = out_ref.at[at, mine]
+        return (pltpu.make_async_remote_copy(half_of, half_of, osend.at[b], orecv.at[b], device_id={"tp": other}, device_id_type=MESH),)
 
     def finish(b, c):
         at = pl.ds(pl.multiple_of(b * size, size), size)
@@ -409,7 +408,7 @@
         for p in range(n_par):
             @pl.when(core == p)
             def _():
-                obuf[at, :] = (x_ref[at, p * half:(p + 1) * half].astype(jnp.float32) + y).astype(jnp.bfloat16)
+                out_ref[at, p * half:(p + 1) * half] = (x_ref[at, p * half:(p + 1) * half].astype(jnp.float32) + y).astype(jnp.bfloat16)
         for copy in out_copies(b):
             copy.start()
         return c
@@ -470,12 +469,12 @@
         out, _, _ = pl.pallas_call(
             functools.partial(layer_kernel, capacity),
             out_shape=(
-                jax.ShapeDtypeStruct((n_tok, d_model), jnp.bfloat16),
+                pltpu.VMEM((n_tok, d_model), jnp.bfloat16),
                 jax.ShapeDtypeStruct((N_HOP[0], cand, d_model), jnp.bfloat16),
                 jax.ShapeDtypeStruct((N_HOP[1], cand, d_model), jnp.bfloat16),
             ),
             in_specs=[vmem_spec, any_spec, any_spec, any_spec],
-            out_specs=(any_spec,) * 3,
+            out_specs=(vmem_spec, any_spec, any_spec),
             scratch_shapes=[
                 pltpu.VMEM((n_tok, d_model), jnp.bfloat16),
                 table, table, table, score, score,
@@ -486,10 +485,10 @@
                 pltpu.VMEM((n_groups, 1, 128), jnp.float32),
                 pltpu.VMEM((2, d_model, hid), jnp.bfloat16), pltpu.VMEM((2, hid, d_model), jnp.bfloat16),
                 pltpu.VMEM((n_groups, own_experts, cand, half), jnp.bfloat16),
-                pltpu.VMEM((n_tok, half), jnp.float32), pltpu.VMEM((n_tok, half), jnp.bfloat16),
+                pltpu.VMEM((n_tok, half), jnp.float32),
                 dma((n_legs,)), dma((n_legs,)), dma((n_jobs,)), dma((n_jobs,)), dma((2,)), dma((2,)), dma((2,)),
                 dma((n_legs,)), dma((n_legs,)), dma((n_groups,)), dma((n_groups,)), dma((n_groups,)), dma((n_groups,)),
-                dma((4,)), dma((4,)), dma((4,)), dma,
+                dma((4,)), dma((4,)), dma,
             ],
             compiler_params=pltpu.CompilerParams(collective_id=0, has_side_effects=True, vmem_limit_bytes=VMEM_LIMIT),
         )(logit_local, x_local, w_up, w_down)

time: 220 us -> 217 us (0.986)
  local copies, waits for them, and re-layouts: 4.79 us -> 2.02 us
    unnamed x1, local copies, waits for them, and re-layouts: 4.79 us -> 2.02 us
where the time goes in v6:
time: 217 us; the launch traced here: 215 us
  Pallas kernels  213 us (98%)
    pallas_call x1, Pallas kernels, local_layer(): pl.pallas_call(functools.partial(layer_kernel, capacity), out_shape=(pltp...  213 us

profile of v6, /device:TPU:1, one launch (start us, length us, event | category | flops | bytes accessed | tf_op | source)
XLA Modules:
  0.0 215.5 jit_solution(8460414139537044222)
XLA Ops:
  0.0 213.4 %shard_map.46 = (bf16[1024,2048]{1,0:T(8,128)(2,1)S(1)}, bf16[54,32,2048]{2,1,0:T(8,128)(2,1)}, bf16[27,32,2048]{2,1,0:T(8,128)(2,1)}) custom-call(f32[1024,128]{1,0:T(8,128)} %logit_ref.1, bf16[1024,2048]{1,0:T(8,128)(2,1)} %x_hbm.1, bf16[2,2048,384]{2,1,0:T(8,128)(2,1)} %wu_ref.1, bf16[2,384,2048]{2,1,0:T(8,128)(2,1)} %wd_ref.1), custom_call_target="tpu_custom_call" | custom-call | tf_op jit(solution)/shard_map/pallas_call | solution.py:469
  213.5 2.0 copy.6

commit v7 on v6

--- a/solution.py
+++ b/solution.py
@@ -10,12 +10,12 @@
 CAP_FACTOR = 2
 MESH = pl.DeviceIdType.MESH
 SIDE = 4
-LAG = 10.0
-EARLY = 8.0
+LAG = 12.0
+EARLY = 10.0
 EARLY_HOP = 8.0
 AHEAD = 2.0
 DONE_LAG = 5.0
-EXPERT_COST = 3.5
+EXPERT_COST = 2.7
 PICK_PER, EXPERT_PER, COMBINE_PER = 8, 8, 4
 VMEM_LIMIT = 59 * 1024 * 1024
 SELF = (0, 0, 0)
@@ -49,8 +49,8 @@
     return sorted(legs), {o: ready[o] - lag for o in jobs}, free
 
 
-OUT_PRIORITY = (47, 11, 14, 4, 51, 20, 56, 18, 1, 48, 62, 29, 44, 16, 37, 30, 10, 19, 12, 33, 63, 49, 9, 17, 25, 5, 32, 50, 36, 15, 57, 38, 52, 53, 2, 3, 21, 23, 8, 22, 26, 45, 7, 31, 59, 27, 43, 46, 54, 42, 55, 28, 35, 41, 6, 39, 58, 40, 61, 60, 24, 13, 34)
-BACK_PRIORITY = (10, 4, 39, 12, 16, 63, 27, 47, 7, 38, 21, 8, 51, 60, 44, 24, 11, 1, 29, 18, 55, 50, 35, 20, 23, 41, 62, 36, 56, 48, 45, 59, 15, 58, 31, 43, 61, 26, 32, 19, 49, 14, 25, 53, 2, 46, 9, 52, 34, 17, 6, 22, 3, 54, 37, 30, 40, 42, 57, 5, 28, 13, 33)
+OUT_PRIORITY = (39, 44, 38, 58, 33, 7, 11, 55, 63, 20, 23, 47, 10, 13, 24, 4, 19, 27, 3, 48, 30, 59, 31, 61, 51, 8, 21, 14, 34, 2, 54, 42, 43, 16, 12, 1, 56, 22, 26, 52, 53, 62, 17, 57, 40, 45, 9, 49, 29, 25, 46, 41, 50, 15, 35, 37, 6, 36, 5, 60, 32, 28, 18)
+BACK_PRIORITY = (23, 12, 36, 29, 4, 25, 31, 13, 28, 42, 57, 8, 33, 46, 18, 51, 20, 2, 45, 62, 7, 55, 3, 21, 6, 17, 43, 59, 53, 32, 63, 9, 40, 26, 54, 48, 14, 39, 19, 1, 50, 27, 35, 52, 16, 37, 38, 10, 41, 24, 15, 60, 61, 58, 49, 30, 44, 56, 11, 47, 22, 34, 5)
 OFFSETS = [(a, b, c) for a in range(SIDE) for b in range(SIDE) for c in range(SIDE) if a or b or c]
 N_LEGS = {o: sum(1 for v in o if v) for o in OFFSETS}
 JOB_ID = {o: j for j, o in enumerate(sorted(OFFSETS, key=lambda o: (-N_LEGS[o], o)))}

time: 217 us -> 214 us (0.986)
  Pallas kernels: 213 us -> 210 us
    pallas_call x1, Pallas kernels: 213 us -> 210 us  [local_layer(): pl.pallas_call(functools.partial(layer_kernel, capacity), out_shape=(pltp...]
where the time goes in v7:
time: 214 us; the launch traced here: 212 us
  Pallas kernels  210 us (98%)
    pallas_call x1, Pallas kernels, local_layer(): pl.pallas_call(functools.partial(layer_kernel, capacity), out_shape=(pltp...  210 us

profile of v7, /device:TPU:1, one launch (start us, length us, event | category | flops | bytes accessed | tf_op | source)
XLA Modules:
  0.0 212.1 jit_solution(6963173479565514613)
XLA Ops:
  0.0 210.0 %shard_map.46 = (bf16[1024,2048]{1,0:T(8,128)(2,1)S(1)}, bf16[54,32,2048]{2,1,0:T(8,128)(2,1)}, bf16[27,32,2048]{2,1,0:T(8,128)(2,1)}) custom-call(f32[1024,128]{1,0:T(8,128)} %logit_ref.1, bf16[1024,2048]{1,0:T(8,128)(2,1)} %x_hbm.1, bf16[2,2048,384]{2,1,0:T(8,128)(2,1)} %wu_ref.1, bf16[2,384,2048]{2,1,0:T(8,128)(2,1)} %wd_ref.1), custom_call_target="tpu_custom_call" | custom-call | tf_op jit(solution)/shard_map/pallas_call | solution.py:469
  210.0 2.0 copy.6
